TPU v7x, 128 devices: a whole 4x4x4 slice. The times are simulated.
128 devices in a mesh: rep: 8 (over y, z_hi), tp: 16 (over z_lo, x, core).
Axes of the slice: x: 4, y: 4, z: 4 (z_hi: 2, z_lo: 2; z = z_hi * 2 + z_lo), core: 2. Of those that a mesh axis runs over, the one named last changes fastest.
Arguments:
- residual: bfloat16 [8, 2048, 4096], P('rep', 'tp'), may hold values from -6 to 6
- gate_pre: bfloat16 [8, 2048, 7168], P('rep', None, 'tp'), may hold values from -6 to 6
- up_pre: bfloat16 [8, 2048, 7168], P('rep', None, 'tp'), may hold values from -6 to 6
- down_weight: bfloat16 [7168, 4096], P('tp'), may hold values from -0.0625 to 0.0625
- d_out: bfloat16 [8, 2048, 4096], P('rep', 'tp'), may hold values from -1.5 to 1.5
- comp_index: int32 [8, 112, 2048], P('rep', 'tp'), may hold values from 0 to 4095
- comp_value: bfloat16 [8, 112, 2048], P('rep', 'tp'), may hold values from -48 to 48
Outputs:
- output: bfloat16 [8, 2048, 4096], P('rep', 'tp')
- gate_preact_gradient: bfloat16 [8, 2048, 7168], P('rep', None, 'tp')
- up_grad: bfloat16 [8, 2048, 7168], P('rep', None, 'tp')
- weight_grad: bfloat16 [8, 7168, 4096], P('rep', 'tp')
- update: bfloat16 [7168, 4096], P('tp')
- updated_down_weight: bfloat16 [7168, 4096], P('tp')
Inputs may be any that keep to these rules, and one draw needn't show every extreme that they name: `comp_index`: positions of one list may repeat.
All inputs are finite; a program needn't handle non-finite values.
Results may differ from a plain program's by a relative error of at most 0.011.
Values may be sent and summed in bfloat16 or wider, within the bound.
No kernel may reach another device: no remote copies, remote signals or barrier semaphores. Data moves between devices by JAX's collectives and lax.ppermute only.
A program may use at most 320 MiB of HBM per device.

v0:
```python
import functools
import math

import jax
import jax.numpy as jnp
import numpy as np
from jax import lax
from jax.experimental import pallas as pl
from jax.experimental.pallas import tpu as pltpu
from jax.sharding import PartitionSpec as P


SPAN = 64
TOPK = 32
LEARN_RATE = 0.02
N_X = 4
N_Y = 4
TOK = 128


NT = (((1,), (1,)), ((), ()))


def tp_of(z, x, c):
    return (z * N_X + x % N_X) * 2 + c


TP = [(z, x, c) for z in range(2) for x in range(N_X) for c in range(2)]
TO_RIGHT = [(tp_of(z, x, c), tp_of(z, x + 1, c)) for z, x, c in TP]
TO_LEFT = [(tp_of(z, x, c), tp_of(z, x - 1, c)) for z, x, c in TP]
TO_Z = [(tp_of(z, x, c), tp_of(1 - z, x, c)) for z, x, c in TP]
TO_CORE = [(tp_of(z, x, c), tp_of(z, x, 1 - c)) for z, x, c in TP]
TO_UP = [(r, (r + 2) % 8) for r in range(8)]
TO_DOWN = [(r, (r - 2) % 8) for r in range(8)]
TO_FAR = [(r, (r + 4) % 8) for r in range(8)]
TO_HI = [(r, r ^ 1) for r in range(8)]
TO_BACK = [(r * 16 + t, (r ^ 1) * 16 + (t ^ 8)) for r in range(8) for t in range(16)]


def right(v):
    return lax.ppermute(v, "tp", TO_RIGHT)


def left(v):
    return lax.ppermute(v, "tp", TO_LEFT)


def over_z(v):
    return lax.ppermute(v, "tp", TO_Z)


def swap(v):
    return lax.ppermute(v, "tp", TO_CORE)


def cosine_table(length):
    freq = np.arange(length)[:, None]
    place = np.arange(length)[None, :]
    scales = np.where(freq == 0, math.sqrt(1.0 / length), math.sqrt(2.0 / length))
    return (scales * np.cos(np.pi * (2.0 * place + 1.0) * freq / (2.0 * length))).astype(np.float32)


def hidden_kernel(spots, g_any, u_any, other_any, own_any, g, u, h, sem_i, sem_o):
    n = g.shape[0]
    width = g.shape[2]
    half = n // 2
    loads = []
    for k in range(n):
        where = (1 - spots[9]) if k < half else spots[9]
        cols = pl.ds(pl.multiple_of(where * (half * width) + (k % half) * width, width), width)
        pair = [
            pltpu.make_async_copy(src.at[:, cols], dst.at[k], sem_i.at[i, k])
            for i, (src, dst) in enumerate(((g_any, g), (u_any, u)))
        ]
        for copy in pair:
            copy.start()
        loads.append(pair)
    stores = []
    for k in range(n):
        for copy in loads[k]:
            copy.wait()
        gf = g[k].astype(jnp.float32)
        h[k] = (gf * jax.nn.sigmoid(gf) * u[k].astype(jnp.float32)).astype(jnp.bfloat16)
        out = other_any if k < half else own_any
        store = pltpu.make_async_copy(h.at[k], out.at[:, (k % half) * width : (k % half + 1) * width], sem_o.at[k])
        store.start()
        stores.append(store)
    for store in stores:
        store.wait()


def hidden_halves(spots, gate_t, up_t):
    units, tokens = gate_t.shape
    n = 4
    any_spec = pl.BlockSpec(memory_space=pl.ANY)
    out = jax.ShapeDtypeStruct((units, tokens // 2), jnp.bfloat16)
    dma = pltpu.SemaphoreType.DMA
    return pl.pallas_call(
        hidden_kernel,
        grid_spec=pltpu.PrefetchScalarGridSpec(
            num_scalar_prefetch=1,
            grid=(),
            in_specs=[any_spec] * 2,
            out_specs=[any_spec] * 2,
            scratch_shapes=[pltpu.VMEM((n, units, tokens // n), jnp.bfloat16)] * 3 + [dma((2, n)), dma((n,))],
        ),
        out_shape=[out, out],
        compiler_params=pltpu.CompilerParams(vmem_limit_bytes=56 << 20),
        cost_estimate=pl.CostEstimate(flops=10 * units * tokens, bytes_accessed=6 * units * tokens, transcendentals=0),
        name="hidden_halves",
    )(spots, gate_t, up_t)


def grads_kernel(first, base, count, idx, *refs):
    refs = list(refs)
    pieces = [[refs.pop(0) for _ in range(n)] for n in count]
    w_any, g_any, u_any = refs.pop(0), refs.pop(0), refs.pop(0)
    if not first:
        acc_any = refs.pop(0)
        refs.pop(0)
        refs.pop(0)
    wg_any, pg_any, ug_any = refs.pop(0), refs.pop(0), refs.pop(0)
    d, w, g, u, acc, pgs, ugs, new = refs[:8]
    sem_d, sem_g, sem_o, sem_w, sem_c = refs[-5:]
    if not first:
        old = refs[8]
    pairs = len(count) // 2
    two = 2 * TOK
    core = idx[8]
    width = w.shape[1]
    chunk = 1024

    def lanes(k):
        return pl.ds(pl.multiple_of(idx[base + k] * two, two), two)

    def load_units(k):
        return (
            pltpu.make_async_copy(g_any.at[:, lanes(k)], g.at[k], sem_g.at[0, k]),
            pltpu.make_async_copy(u_any.at[:, lanes(k)], u.at[k], sem_g.at[1, k]),
        )

    def store_units(k):
        return (
            pltpu.make_async_copy(pgs.at[k], pg_any.at[:, lanes(k)], sem_o.at[0, k]),
            pltpu.make_async_copy(ugs.at[k], ug_any.at[:, lanes(k)], sem_o.at[1, k]),
        )

    weights = pltpu.make_async_copy(w_any, w, sem_w.at[0])
    if not first:
        before = pltpu.make_async_copy(acc_any, old, sem_w.at[1])

    def load_pair(k):
        for copy in load_units(k):
            copy.start()
        for side in range(2):
            at = 0
            where = core if side == 0 else 1 - core
            for piece in pieces[2 * k + side]:
                size = piece.shape[0]
                there = pl.ds(pl.multiple_of(k * two + where * TOK + at, 64), size)
                pltpu.make_async_copy(piece, d.at[there, :], sem_d.at[k, side]).start()
                at += size

    load_pair(0)
    weights.start()

    def wait_pair(k):
        for copy in load_units(k):
            copy.wait()
        for side in range(2):
            there = pl.ds(pl.multiple_of(k * two + side * TOK, TOK), TOK)
            pltpu.make_async_copy(w_any.at[0:TOK, :], d.at[there, :], sem_d.at[k, side]).wait()

    def units_of(k):
        gf = g[k].astype(jnp.float32)
        uf = u[k].astype(jnp.float32)
        s = jax.nn.sigmoid(gf)
        return gf, uf, s, gf * s

    def to_inputs(k, h, gf, uf, s, act):
        pgs[k] = (h * uf * s * (1.0 + gf * (1.0 - s))).astype(jnp.bfloat16)
        ugs[k] = (h * act).astype(jnp.bfloat16)
        for copy in store_units(k):
            copy.start()

    def one(k, _):
        wait_pair(k)
        for n in range(1, pairs):

            @pl.when(k == n - 1)
            def _(n=n):
                load_pair(n)
                if n == pairs - 1 and not first:
                    before.start()

        rows = pl.ds(pl.multiple_of(k * two, two), two)
        gf, uf, s, act = units_of(k)
        hid = (act * uf).astype(jnp.bfloat16)
        h = lax.dot_general(w[...], d[rows, :], NT, preferred_element_type=jnp.float32)
        for c in range(0, width, chunk):
            cols = slice(c, c + chunk)
            acc[:, cols] += jnp.dot(hid, d[rows, cols], preferred_element_type=jnp.float32)
        to_inputs(k, h, gf, uf, s, act)
        return 0

    acc[...] = jnp.zeros_like(acc)
    weights.wait()
    lax.fori_loop(0, pairs - 1, one, 0)
    k = pairs - 1
    wait_pair(k)
    if not first:
        before.wait()
    rows = slice(k * two, (k + 1) * two)
    gf, uf, s, act = units_of(k)
    hid = (act * uf).astype(jnp.bfloat16)
    stores = []
    for n, c in enumerate(range(0, width, chunk)):
        cols = slice(c, c + chunk)
        total = acc[:, cols] + jnp.dot(hid, d[rows, cols], preferred_element_type=jnp.float32)
        if not first:
            total = total + old[:, cols].astype(jnp.float32)
        new[:, cols] = total.astype(jnp.bfloat16)
        copy = pltpu.make_async_copy(new.at[:, cols], wg_any.at[:, cols], sem_c.at[n])
        copy.start()
        stores.append(copy)
    h = lax.dot_general(w[...], d[rows, :], NT, preferred_element_type=jnp.float32)
    to_inputs(k, h, gf, uf, s, act)
    for k in range(pairs):
        stores += store_units(k)
    for copy in stores:
        copy.wait()


def grads(base, idx, shards, w, gate_t, up_t, before=None):
    units, tokens = gate_t.shape
    width = w.shape[1]
    first = before is None
    count = [len(s) for s in shards]
    pairs = len(count) // 2
    two = 2 * TOK
    any_spec = pl.BlockSpec(memory_space=pl.ANY)
    args = [idx, *[v for s in shards for v in s], w, gate_t, up_t]
    aliases = {}
    bf, f32 = jnp.bfloat16, jnp.float32
    if not first:
        aliases = {len(args) + 1: 1, len(args) + 2: 2}
        args += list(before)
    scratch = [
        pltpu.VMEM((pairs * two, width), bf),
        pltpu.VMEM((units, width), bf),
        pltpu.VMEM((pairs, units, two), bf),
        pltpu.VMEM((pairs, units, two), bf),
        pltpu.VMEM((units, width), f32),
        pltpu.VMEM((pairs, units, two), bf),
        pltpu.VMEM((pairs, units, two), bf),
        pltpu.VMEM((units, width), bf),
    ]
    if not first:
        scratch += [pltpu.VMEM((units, width), bf)]
    dma = pltpu.SemaphoreType.DMA
    scratch += [dma((pairs, 2)), dma((2, pairs)), dma((2, pairs)), dma((2,)), dma((width // 1024,))]
    flat = jax.ShapeDtypeStruct((units, tokens), bf)
    return pl.pallas_call(
        functools.partial(grads_kernel, first, base, count),
        grid_spec=pltpu.PrefetchScalarGridSpec(
            num_scalar_prefetch=1,
            grid=(),
            in_specs=[any_spec] * (len(args) - 1),
            out_specs=[any_spec] * 3,
            scratch_shapes=scratch,
        ),
        out_shape=[jax.ShapeDtypeStruct((units, width), bf), flat, flat],
        input_output_aliases=aliases,
        compiler_params=pltpu.CompilerParams(vmem_limit_bytes=56 << 20),
        cost_estimate=pl.CostEstimate(flops=4 * units * width * pairs * two, bytes_accessed=24 << 20, transcendentals=0),
        name="grads_first" if first else "grads_second",
    )(*args)


def forward_kernel(count, pos, *refs):
    refs = list(refs)
    hiddens = [refs.pop(0) for _ in range(4)]
    w_refs = [refs.pop(0) for _ in range(count)]
    outs = [refs.pop(0) for _ in range(8)]
    lhs_t, lhs, w, out, sem_h, sem_w, sem_o = refs
    units = w_refs[0].shape[0]
    quarter = units // N_Y
    width = w_refs[0].shape[1] // 2
    bn = width // 2
    gets = []
    for r in range(4):
        cols = slice(r * TOK, (r + 1) * TOK)
        there = pl.ds(pl.multiple_of(pos[10 + r] * TOK, TOK), TOK)
        for n in range(2):
            to = lhs_t.at[n * units : (n + 1) * units, cols]
            gets.append(pltpu.make_async_copy(hiddens[n].at[:, there], to, sem_h.at[r, n]))
            for q in range(N_Y):
                base = (2 + n) * units + q * quarter
                rows = pl.ds(pl.multiple_of(pos[14 + q] * quarter, 16), quarter)
                to = lhs_t.at[base : base + quarter, cols]
                gets.append(pltpu.make_async_copy(hiddens[2 + n].at[rows, there], to, sem_h.at[r, 2 + N_Y * n + q]))
    for get in gets:
        get.start()
    loads = []
    for piece in range(4):
        at = 0
        cols = slice(piece * bn, (piece + 1) * bn)
        mine = []
        for n, r in enumerate(w_refs):
            mine.append(pltpu.make_async_copy(r.at[:, cols], w.at[piece, at : at + r.shape[0], :], sem_w.at[piece, n]))
            at += r.shape[0]
        loads.append(mine)
    for load in loads[0]:
        load.start()
    for get in gets:
        get.wait()
    lhs[...] = lhs_t[...].T
    puts = []
    step = 512
    for piece in range(4):
        half, off = piece // 2, piece % 2 * bn
        for load in loads[piece]:
            load.wait()
        if piece < 3:
            for load in loads[piece + 1]:
                load.start()

        def tile(j, _, piece=piece, half=half, off=off):
            here = pl.ds(pl.multiple_of(j * step, step), step)
            there = pl.ds(pl.multiple_of(off + j * step, step), step)
            out[half, :, there] = jnp.dot(lhs[...], w[piece, :, here], preferred_element_type=jnp.float32).astype(jnp.bfloat16)
            return 0

        lax.fori_loop(0, bn // step, tile, 0)
        for r in range(4):
            cols = slice(off, off + bn)
            put = pltpu.make_async_copy(
                out.at[half, r * TOK : (r + 1) * TOK, cols], outs[4 * half + r].at[:, cols], sem_o.at[piece, r]
            )
            put.start()
            puts.append(put)
    for put in puts:
        put.wait()


def forward(pos, hiddens, weights):
    units, _ = hiddens[0].shape
    width = weights[0].shape[1] // 2
    any_spec = pl.BlockSpec(memory_space=pl.ANY)
    part = jax.ShapeDtypeStruct((TOK, width), jnp.bfloat16)
    bf = jnp.bfloat16
    dma = pltpu.SemaphoreType.DMA
    parts = pl.pallas_call(
        functools.partial(forward_kernel, len(weights)),
        grid_spec=pltpu.PrefetchScalarGridSpec(
            num_scalar_prefetch=1,
            grid=(),
            in_specs=[any_spec] * (4 + len(weights)),
            out_specs=[any_spec] * 8,
            scratch_shapes=[
                pltpu.VMEM((4 * units, 4 * TOK), bf),
                pltpu.VMEM((4 * TOK, 4 * units), bf),
                pltpu.VMEM((4, 4 * units, width // 2), bf),
                pltpu.VMEM((2, 4 * TOK, width), bf),
                dma((4, 2 + 2 * N_Y)),
                dma((4, len(weights))),
                dma((4, 4)),
            ],
        ),
        out_shape=[part] * 8,
        compiler_params=pltpu.CompilerParams(vmem_limit_bytes=56 << 20),
        cost_estimate=pl.CostEstimate(flops=2 * 4 * TOK * 4 * units * 2 * width, bytes_accessed=22 << 20, transcendentals=0),
        name="forward",
    )(pos, *hiddens, *weights)
    return parts[:4], parts[4:]


def decode_kernel(comp_a, comp_b, comp_c, comp_d, wv, cos_ref, ct_ref, upv, newv, cb_ref, fields, co4, mid):
    bf, f32 = jnp.bfloat16, jnp.float32
    a = pl.program_id(0)
    comps = [ref.at[n] for ref in (comp_a, comp_b, comp_c, comp_d) for n in range(ref.shape[0])]
    replicas = len(comps)
    per = 128 // TOPK
    groups = fields.shape[2]
    rows = fields.shape[1] // 3
    count = replicas * TOPK

    @pl.when(a == 0)
    def _():
        cb_ref[...] = jnp.zeros_like(cb_ref)
        for bl in range(per):
            here = slice(bl * SPAN, (bl + 1) * SPAN)
            cb_ref[here, here] = cos_ref[...]
        lane = lax.broadcasted_iota(jnp.int32, (128, count), 0)
        out = lax.broadcasted_iota(jnp.int32, (128, count), 1)
        for bl in range(per):
            total = None
            for r in range(replicas):
                pick = ((lane == bl * TOPK + out - r * TOPK) & (out // TOPK == r)).astype(f32).astype(bf)
                part = jnp.dot(comps[r][...], pick, preferred_element_type=f32)
                total = part if total is None else total + part
            fields[bl] = total.reshape(fields.shape[1:])

    spot = lax.broadcasted_iota(jnp.int32, (SPAN, count), 0).astype(f32)

    def group(g, _):
        four = []
        for bl in range(per):
            at = pl.ds(g, 1)
            i = fields[bl, a, at, :]
            j = fields[bl, rows + a, at, :]
            v = fields[bl, 2 * rows + a, at, :]
            left_hot = jnp.where(spot == i, v, 0.0).astype(bf)
            right_hot = jnp.where(spot == j, 1.0, 0.0).astype(bf)
            four.append(lax.dot_general(left_hot, right_hot, NT, preferred_element_type=f32))
        co4[pl.ds(pl.multiple_of(g * SPAN, SPAN), SPAN), :] = jnp.concatenate(four, axis=1).astype(bf)
        return 0

    lax.fori_loop(0, groups, group, 0, unroll=16)
    mid[...] = jnp.dot(co4[...], cb_ref[...], preferred_element_type=f32).astype(bf)
    step = per * SPAN
    for g in range(groups):
        cols = slice(g * step, (g + 1) * step)
        block = jnp.dot(ct_ref[...], mid[g * SPAN : (g + 1) * SPAN, :], preferred_element_type=f32)
        update = block.astype(bf)
        upv[:, cols] = update
        newv[:, cols] = (wv[:, cols].astype(f32) - LEARN_RATE * update.astype(f32)).astype(bf)


def decode(comp, w):
    replicas = sum(v.shape[0] for v in comp)
    width = w.shape[1]
    rows = w.shape[0] // SPAN
    per = 128 // TOPK
    groups = width // SPAN // per
    cos = cosine_table(SPAN)
    cb = jnp.asarray(cos, jnp.bfloat16)
    ct = jnp.asarray(cos.T / replicas, jnp.bfloat16)
    whole = lambda v: pl.BlockSpec(v.shape, lambda a: (0,) * v.ndim)
    wide = pl.BlockSpec((SPAN, width), lambda a: (a, 0))
    out = jax.ShapeDtypeStruct(w.shape, jnp.bfloat16)
    bf = jnp.bfloat16
    return pl.pallas_call(
        decode_kernel,
        grid=(rows,),
        in_specs=[*[whole(v) for v in comp], wide, whole(cb), whole(ct)],
        out_specs=[wide, wide],
        out_shape=[out, out],
        scratch_shapes=[
            pltpu.VMEM((per * SPAN, per * SPAN), bf),
            pltpu.VMEM((per, 3 * rows, groups, replicas * TOPK), jnp.float32),
            pltpu.VMEM((groups * SPAN, per * SPAN), bf),
            pltpu.VMEM((groups * SPAN, per * SPAN), bf),
        ],
        cost_estimate=pl.CostEstimate(flops=8 << 30, bytes_accessed=12 << 20, transcendentals=0),
        name="decode",
    )(*comp, w, cb, ct)


def everyones_components(comp_index, comp_value):
    index = comp_index[0]
    mine = jnp.concatenate(
        [(index // SPAN).astype(jnp.bfloat16), (index % SPAN).astype(jnp.bfloat16), comp_value[0]], axis=0
    )
    mine = mine.reshape(-1, 128)
    pair = jnp.stack([mine, lax.ppermute(mine, "rep", TO_HI)])
    return [pair] + [lax.ppermute(pair, "rep", to) for to in (TO_UP, TO_DOWN, TO_FAR)]


def body(residual, gate_pre, up_pre, down_weight, d_out, comp_index, comp_value):
    t = lax.axis_index("tp")
    z, x, c = t // (2 * N_X), (t // 2) % N_X, t % 2
    y = lax.axis_index("rep") // 2
    gate_t = jnp.swapaxes(gate_pre[0], 0, 1)
    up_t = jnp.swapaxes(up_pre[0], 0, 1)
    w = down_weight
    quarter = w.shape[0] // N_Y
    own = d_out[0]

    steps = ((0, 0), (1, 0), (0, 3), (0, 1), (0, 2), (1, 3), (1, 1), (1, 2))
    spots = jnp.stack(
        [(z if dz == 0 else 1 - z) * N_X + (x + dx) % N_X for dz, dx in steps]
        + [c, z]
        + [((x + r) % N_X) * 2 + c for r in (2, 1, 3, 0)]
        + [(y + q) % N_Y for q in (0, 3, 1, 2)]
    ).astype(jnp.int32)

    from_z = over_z(own)
    from_l = right(own)
    from_r = left(own)
    own_p = swap(own)
    w_q0 = lax.ppermute(lax.dynamic_slice_in_dim(w, y * quarter, quarter, 0), ("rep", "tp"), TO_BACK)
    far_q = (y + N_Y // 2) % N_Y
    w_q2 = lax.ppermute(lax.dynamic_slice_in_dim(w, far_q * quarter, quarter, 0), ("rep", "tp"), TO_BACK)
    w_p = swap(w)
    comp = everyones_components(comp_index, comp_value)
    hid_other, hid_own = hidden_halves(spots, gate_t, up_t)
    hz = over_z(hid_other)
    hs_p = swap(hid_own)
    hz_p = swap(hz)

    update, updated = decode(comp, w)

    half_rows = TOK // 2
    cut_a = from_l[:half_rows]
    cut_b = from_r[half_rows:]
    far_a = right(cut_a)
    far_b = left(cut_b)
    from_zl = right(from_z)
    from_zr = left(from_z)
    from_zfar_a = over_z(far_a)
    from_zfar_b = over_z(far_b)

    near = [[own], [own_p], [from_z], [swap(from_z)]]
    near += [[from_l], [swap(from_l)], [from_r], [swap(from_r)]]
    before = grads(0, spots, near, w, gate_t, up_t)
    rest = [[far_a, far_b], [swap(far_a), swap(far_b)]]
    rest += [[from_zl], [swap(from_zl)], [from_zr], [swap(from_zr)]]
    rest += [[from_zfar_a, from_zfar_b], [swap(from_zfar_a), swap(from_zfar_b)]]
    weight_grad, pre_grad, up_grad = grads(
        4, spots, rest, w, gate_t, up_t, before
    )

    width = w.shape[1] // 2
    w_qm = lax.ppermute(w_q0, "rep", TO_UP)
    w_qp = lax.ppermute(w_q0, "rep", TO_DOWN)
    w_back = [w_q0, w_qm, w_qp, w_q2]
    weights = [w, w_p, *w_back, *[swap(v) for v in w_back]]
    (a2, a1, a3, a0), (b2, b1, b3, b0) = forward(spots, (hid_own, hs_p, hz, hz_p), weights)
    f32 = jnp.float32

    ra = right(a2)
    rb = left(b2)
    ga = left(a3)
    gb = right(b1)
    sum_a = (a1.astype(f32) + ra.astype(f32)).astype(jnp.bfloat16)
    sum_b = (b3.astype(f32) + rb.astype(f32)).astype(jnp.bfloat16)
    fa = right(sum_a)
    fb = left(sum_b)
    res = residual[0]
    out_a = res[:, :width].astype(f32) + a0.astype(f32) + ga.astype(f32) + fa.astype(f32)
    out_b = res[:, width:].astype(f32) + b0.astype(f32) + gb.astype(f32) + fb.astype(f32)
    output = jnp.concatenate([out_a, out_b], axis=1).astype(jnp.bfloat16)
    return (
        output[None],
        jnp.swapaxes(pre_grad, 0, 1)[None],
        jnp.swapaxes(up_grad, 0, 1)[None],
        weight_grad[None],
        update,
        updated,
    )


def solution(mesh):
    return jax.shard_map(
        body,
        mesh=mesh,
        in_specs=(
            P("rep", "tp", None),
            P("rep", None, "tp"),
            P("rep", None, "tp"),
            P("tp", None),
            P("rep", "tp", None),
            P("rep", "tp", None),
            P("rep", "tp", None),
        ),
        out_specs=(
            P("rep", "tp", None),
            P("rep", None, "tp"),
            P("rep", None, "tp"),
            P("rep", "tp", None),
            P("tp", None),
            P("tp", None),
        ),
        check_vma=False,
    )
```

profile of v0, /device:TPU:0, one launch (start us, length us, event | category | flops | bytes accessed | tf_op | source)
XLA Modules:
  0.0 211.1 jit_solution(9197592254507716699)
XLA Ops:
  0.8 0.7 stack.81.spots.pos.idx
  1.5 3.7 %hidden_halves.1 = (bf16[448,1024]{1,0:T(8,128)(2,1)}, bf16[448,1024]{1,0:T(8,128)(2,1)}) custom-call(s32[18]{0:T(128)} %stack.81.spots.pos.idx, bf16[448,2048]{1,0:T(8,128)(2,1)} %bitcast.65, bf16[448,2048]{1,0:T(8,128)(2,1)} %bitcast.68), custom_call_target="tpu_custom_call" | custom-call | flops 9175040 | bytes 5505024 | tf_op jit(solution)/shard_map/hidden_halves/pallas_call | solution.py:98
  5.3 2.1 collective-permute-start.1
  7.7 3.7 %collective-permute-start.37 = (bf16[336,128]{1,0:T(8,128)(2,1)S(1)}, bf16[336,128]{1,0:T(8,128)(2,1)S(1)}, u32[]{:S(2)}, u32[]{:S(2)}) collective-permute-start(bf16[336,128]{1,0:T(8,128)(2,1)S(1)} %reshape.46), channel_id=1, source_target_pairs={{0,16},{16,0},{32,48},{48,32},{64,80},{80,64},{96,112},{112,96},{1... | collective-permute-start | bytes 258056 | tf_op jit(solution)/shard_map/ppermute | solution.py:466
  11.3 1.6 constant_dynamic-slice_fusion
  13.1 20.7 %collective-permute-done.37 = bf16[336,128]{1,0:T(8,128)(2,1)S(1)} collective-permute-done((bf16[336,128]{1,0:T(8,128)(2,1)S(1)}, bf16[336,128]{1,0:T(8,128)(2,1)S(1)}, u32[]{:S(2)}, u32[]{:S(2)}) %collective-permute-start.37) | collective-permute-done | bytes 86048 | tf_op jit(solution)/shard_map/ppermute | solution.py:466
  33.8 1.6 collective-permute-start.38
  35.5 1.5 collective-permute-start.18
  37.0 3.9 %collective-permute-done.38.comp_b = bf16[2,336,128]{2,1,0:T(8,128)(2,1)S(1)} collective-permute-done((bf16[2,336,128]{2,1,0:T(8,128)(2,1)S(1)}, bf16[2,336,128]{2,1,0:T(8,128)(2,1)S(1)}, u32[]{:S(2)}, u32[]{:S(2)}) %collective-permute-start.38) | collective-permute-done | bytes 172064 | tf_op jit(solution)/shard_map/ppermute | solution.py:467
  40.9 1.7 collective-permute-start.39
  42.7 3.7 %collective-permute-done.39.comp_c = bf16[2,336,128]{2,1,0:T(8,128)(2,1)S(1)} collective-permute-done((bf16[2,336,128]{2,1,0:T(8,128)(2,1)S(1)}, bf16[2,336,128]{2,1,0:T(8,128)(2,1)S(1)}, u32[]{:S(2)}, u32[]{:S(2)}) %collective-permute-start.39) | collective-permute-done | bytes 172064 | tf_op jit(solution)/shard_map/ppermute | solution.py:467
  46.3 1.9 collective-permute-start.40
  48.3 5.0 %collective-permute-done.40.comp_d = bf16[2,336,128]{2,1,0:T(8,128)(2,1)S(1)} collective-permute-done((bf16[2,336,128]{2,1,0:T(8,128)(2,1)S(1)}, bf16[2,336,128]{2,1,0:T(8,128)(2,1)S(1)}, u32[]{:S(2)}, u32[]{:S(2)}) %collective-permute-start.40) | collective-permute-done | bytes 172064 | tf_op jit(solution)/shard_map/ppermute | solution.py:467
  53.3 2.8 %collective-permute-start.20 = (bf16[128,4096]{1,0:T(8,128)(2,1)}, bf16[128,4096]{1,0:T(8,128)(2,1)}, u32[]{:S(2)}, u32[]{:S(2)}) collective-permute-start(bf16[128,4096]{1,0:T(8,128)(2,1)} %bitcast.75), channel_id=1, source_target_pairs={{0,6},{1,7},{2,0},{3,1},{4,2},{5,3},{6,4},{7,5},{8,14},{9,15},{10,... | collective-permute-start | bytes 3145736 | tf_op jit(solution)/shard_map/ppermute | solution.py:45
  56.0 0.5 collective-permute-start.7
  56.5 4.6 %collective-permute-done.18.refs_4_ = bf16[128,4096]{1,0:T(8,128)(2,1)S(1)} collective-permute-done((bf16[128,4096]{1,0:T(8,128)(2,1)}, bf16[128,4096]{1,0:T(8,128)(2,1)S(1)}, u32[]{:S(2)}, u32[]{:S(2)}) %collective-permute-start.18) | collective-permute-done | bytes 1048608 | tf_op jit(solution)/shard_map/ppermute | solution.py:41
  61.2 14.4 %collective-permute-done.20.refs_6_ = bf16[128,4096]{1,0:T(8,128)(2,1)} collective-permute-done((bf16[128,4096]{1,0:T(8,128)(2,1)}, bf16[128,4096]{1,0:T(8,128)(2,1)}, u32[]{:S(2)}, u32[]{:S(2)}) %collective-permute-start.20) | collective-permute-done | bytes 1048608 | tf_op jit(solution)/shard_map/ppermute | solution.py:45
  75.6 1.1 slice.19
  76.7 1.4 collective-permute-start.19
  78.1 2.6 %collective-permute-start.21 = (bf16[64,4096]{1,0:T(8,128)(2,1)S(1)}, bf16[64,4096]{1,0:T(8,128)(2,1)}, u32[]{:S(2)}, u32[]{:S(2)}) collective-permute-start(bf16[64,4096]{1,0:T(8,128)(2,1)S(1)} %slice.19), channel_id=1, source_target_pairs={{0,6},{1,7},{2,0},{3,1},{4,2},{5,3},{6,4},{7,5},{8,14},{9,15},{10,... | collective-permute-start | bytes 1572872 | tf_op jit(solution)/shard_map/ppermute | solution.py:45
  81.0 12.1 %collective-permute-done.19.refs_0_ = bf16[64,4096]{1,0:T(8,128)(2,1)S(1)} collective-permute-done((bf16[64,4096]{1,0:T(8,128)(2,1)S(1)}, bf16[64,4096]{1,0:T(8,128)(2,1)S(1)}, u32[]{:S(2)}, u32[]{:S(2)}) %collective-permute-start.19) | collective-permute-done | bytes 524320 | tf_op jit(solution)/shard_map/ppermute | solution.py:41
  93.2 2.7 %collective-permute-start.6 = (bf16[112,4096]{1,0:T(8,128)(2,1)}, bf16[112,4096]{1,0:T(8,128)(2,1)S(1)}, u32[]{:S(2)}, u32[]{:S(2)}) collective-permute-start(bf16[112,4096]{1,0:T(8,128)(2,1)} %collective-permute-done.4.refs_6_), channel_id=1, source_target_pairs={{0,96},{16,112},{32,0},{48,16},{64,32},{80,48},{96,64},{112,80},{1... | collective-permute-start | bytes 2752520 | tf_op jit(solution)/shard_map/ppermute | solution.py:526
  95.9 0.5 collective-permute-start.11
  96.4 8.2 %collective-permute-done.5.refs_7_ = bf16[112,4096]{1,0:T(8,128)(2,1)S(1)} collective-permute-done((bf16[112,4096]{1,0:T(8,128)(2,1)}, bf16[112,4096]{1,0:T(8,128)(2,1)S(1)}, u32[]{:S(2)}, u32[]{:S(2)}) %collective-permute-start.5) | collective-permute-done | bytes 917536 | tf_op jit(solution)/shard_map/ppermute | solution.py:525
  104.6 11.3 %collective-permute-done.6.refs_8_ = bf16[112,4096]{1,0:T(8,128)(2,1)S(1)} collective-permute-done((bf16[112,4096]{1,0:T(8,128)(2,1)}, bf16[112,4096]{1,0:T(8,128)(2,1)S(1)}, u32[]{:S(2)}, u32[]{:S(2)}) %collective-permute-start.6) | collective-permute-done | bytes 917536 | tf_op jit(solution)/shard_map/ppermute | solution.py:526
  115.9 0.5 collective-permute-start.10
  116.5 3.9 %collective-permute-done.22.refs_2_ = bf16[64,4096]{1,0:T(8,128)(2,1)S(1)} collective-permute-done((bf16[64,4096]{1,0:T(8,128)(2,1)S(1)}, bf16[64,4096]{1,0:T(8,128)(2,1)S(1)}, u32[]{:S(2)}, u32[]{:S(2)}) %collective-permute-start.22) | collective-permute-done | bytes 524320 | tf_op jit(solution)/shard_map/ppermute | solution.py:53
  120.4 1.6 collective-permute-start.27
  122.0 8.4 %collective-permute-done.25.refs_4_ = bf16[128,4096]{1,0:T(8,128)(2,1)S(1)} collective-permute-done((bf16[128,4096]{1,0:T(8,128)(2,1)}, bf16[128,4096]{1,0:T(8,128)(2,1)S(1)}, u32[]{:S(2)}, u32[]{:S(2)}) %collective-permute-start.25) | collective-permute-done | bytes 1048608 | tf_op jit(solution)/shard_map/ppermute | solution.py:41
  130.5 0.6 collective-permute-start.35
  131.4 0.9 copy-done.20
  132.4 0.4 collective-permute-start.36
  132.8 12.9 %decode.1 = (bf16[448,4096]{1,0:T(8,128)(2,1)}, bf16[448,4096]{1,0:T(8,128)(2,1)}) custom-call(bf16[2,336,128]{2,1,0:T(8,128)(2,1)} %copy-done.6, bf16[2,336,128]{2,1,0:T(8,128)(2,1)} %copy-done.28, bf16[2,336,128]{2,1,0:T(8,128)(2,1)} %copy-done.29, bf16[2,336,128]{2,1,0:T(8,128)(2,1)} %copy-done.30, bf16[448,4096]{1,0:T(8,128)(2,1)} %wv.1, ...), custom_call_target="tpu_custom_call" | custom-call | flops 8589934592 | bytes 12582912 | tf_op jit(solution)/shard_map/decode/pallas_call | solution.py:443
  145.8 14.7 %forward.1 = (bf16[128,2048]{1,0:T(8,128)(2,1)}, bf16[128,2048]{1,0:T(8,128)(2,1)}, bf16[128,2048]{1,0:T(8,128)(2,1)}, bf16[128,2048]{1,0:T(8,128)(2,1)}, bf16[1...) custom-call(s32[18]{0:T(128)} %stack.81.spots.pos.idx, ...), custom_call_target="tpu_custom_call" | custom-call | flops 7516192768 | bytes 23068672 | tf_op jit(solution)/shard_map/forward/pallas_call | solution.py:353
  160.5 2.1 collective-permute-start.30
  162.6 0.5 collective-permute-start.28
  163.1 3.2 %collective-permute-start.16 = (bf16[128,2048]{1,0:T(8,128)(2,1)}, bf16[128,2048]{1,0:T(8,128)(2,1)S(1)}, u32[]{:S(2)}, u32[]{:S(2)}) collective-permute-start(bf16[128,2048]{1,0:T(8,128)(2,1)} %get-tuple-element.33), channel_id=1, source_target_pairs={{0,6},{1,7},{2,0},{3,1},{4,2},{5,3},{6,4},{7,5},{8,14},{9,15},{10,... | collective-permute-start | bytes 1572872 | tf_op jit(solution)/shard_map/ppermute | solution.py:45
  166.4 13.5 %grads_first.1 = (bf16[448,4096]{1,0:T(8,128)(2,1)}, bf16[448,2048]{1,0:T(8,128)(2,1)}, bf16[448,2048]{1,0:T(8,128)(2,1)}) custom-call(s32[18]{0:T(128)} %stack.81.spots.pos.idx, bf16[128,4096]{1,0:T(8,128)(2,1)} %bitcast.78, bf16[128,4096]{1,0:T(8,128)(2,1)} %copy-done.10, bf16[128,4096]{1,0:T(8,128)(2,1)} %collective-permute-done.24.refs_2_, ...), custom_call_target="tpu_custom_call" | custom-call | flops 7516192768 | bytes 25165824 | tf_op jit(solution)/shard_map/grads_first/pallas_call | solution.py:263
  180.0 0.5 collective-permute-start.31
  180.8 1.2 collective-permute-done.23.refs_3_
  182.2 0.6 collective-permute-done.31.refs_10_
  182.8 1.3 collective-permute-start.15
  184.3 3.5 %collective-permute-start.17 = (bf16[128,2048]{1,0:T(8,128)(2,1)S(1)}, bf16[128,2048]{1,0:T(8,128)(2,1)S(1)}, u32[]{:S(2)}, u32[]{:S(2)}) collective-permute-start(bf16[128,2048]{1,0:T(8,128)(2,1)S(1)} %add_convert_fusion.1), channel_id=1, source_target_pairs={{0,6},{1,7},{2,0},{3,1},{4,2},{5,3},{6,4},{7,5},{8,14},{9,15},{10,... | collective-permute-start | bytes 1572872 | tf_op jit(solution)/shard_map/ppermute | solution.py:45
  187.8 1.0 copy-done.12
  188.7 15.4 %grads_second.1 = (bf16[448,4096]{1,0:T(8,128)(2,1)}, bf16[448,2048]{1,0:T(8,128)(2,1)}, bf16[448,2048]{1,0:T(8,128)(2,1)}) custom-call(s32[18]{0:T(128)} %stack.81.spots.pos.idx, bf16[64,4096]{1,0:T(8,128)(2,1)} %copy-done.21, bf16[64,4096]{1,0:T(8,128)(2,1)} %collective-permute-done.21.refs_1_, ...), custom_call_target="tpu_custom_call", output_to_operand_aliasing={{1}: (17, {}), {2}: (18, {})} | custom-call | flops 7516192768 | bytes 25165824 | tf_op jit(solution)/shard_map/grads_second/pallas_call | solution.py:263
  204.1 5.1 %collective-permute-done.14 = bf16[128,2048]{1,0:T(8,128)(2,1)S(1)} collective-permute-done((bf16[128,2048]{1,0:T(8,128)(2,1)S(1)}, bf16[128,2048]{1,0:T(8,128)(2,1)S(1)}, u32[]{:S(2)}, u32[]{:S(2)}) %collective-permute-start.14) | collective-permute-done | bytes 524320 | tf_op jit(solution)/shard_map/ppermute | solution.py:41
  209.3 0.8 fusion
  210.0 1.1 pad_maximum_fusion
  (114 shorter events, 2.3 us)
Async XLA Ops:
  5.2 50.8 %collective-permute-start = (bf16[448,1024]{1,0:T(8,128)(2,1)}, bf16[448,1024]{1,0:T(8,128)(2,1)}, u32[]{:S(2)}, u32[]{:S(2)}) collective-permute-start(bf16[448,1024]{1,0:T(8,128)(2,1)} %get-tuple-element.24.refs_0_), channel_id=1, source_target_pairs={{0,1},{1,0},{2,3},{3,2},{4,5},{5,4},{6,7},{7,6},{8,9},{9,8},{10,11... | collective-permute-start | bytes 2752520 | tf_op jit(solution)/shard_map/ppermute | solution.py:53
  5.3 50.7 %collective-permute-start.1 = (bf16[448,1024]{1,0:T(8,128)(2,1)}, bf16[448,1024]{1,0:T(8,128)(2,1)}, u32[]{:S(2)}, u32[]{:S(2)}) collective-permute-start(bf16[448,1024]{1,0:T(8,128)(2,1)} %get-tuple-element.25), channel_id=1, source_target_pairs={{0,8},{1,9},{2,10},{3,11},{4,12},{5,13},{6,14},{7,15},{8,0},{9,1},... | collective-permute-start | bytes 2752520 | tf_op jit(solution)/shard_map/ppermute | solution.py:49
  7.7 26.2 %collective-permute-start.37 = (bf16[336,128]{1,0:T(8,128)(2,1)S(1)}, bf16[336,128]{1,0:T(8,128)(2,1)S(1)}, u32[]{:S(2)}, u32[]{:S(2)}) collective-permute-start(bf16[336,128]{1,0:T(8,128)(2,1)S(1)} %reshape.46), channel_id=1, source_target_pairs={{0,16},{16,0},{32,48},{48,32},{64,80},{80,64},{96,112},{112,96},{1... | collective-permute-start | bytes 258056 | tf_op jit(solution)/shard_map/ppermute | solution.py:466
  12.9 43.6 %collective-permute-start.4 = (bf16[112,4096]{1,0:T(8,128)(2,1)S(1)}, bf16[112,4096]{1,0:T(8,128)(2,1)}, u32[]{:S(2)}, u32[]{:S(2)}) collective-permute-start(bf16[112,4096]{1,0:T(8,128)(2,1)S(1)} %get-tuple-element.43), channel_id=1, source_target_pairs={{0,24},{1,25},{2,26},{3,27},{4,28},{5,29},{6,30},{7,31},{8,16},{9,... | collective-permute-start | bytes 2752520 | tf_op jit(solution)/shard_map/ppermute | solution.py:492
  33.8 98.9 %copy-start.6 = (bf16[2,336,128]{2,1,0:T(8,128)(2,1)}, bf16[2,336,128]{2,1,0:T(8,128)(2,1)S(1)}, u32[]{:S(2)}) copy-start(bf16[2,336,128]{2,1,0:T(8,128)(2,1)S(1)} %pad_maximum_fusion.1.comp_a) | copy-start | bytes 516100
  33.8 7.1 %collective-permute-start.38 = (bf16[2,336,128]{2,1,0:T(8,128)(2,1)S(1)}, bf16[2,336,128]{2,1,0:T(8,128)(2,1)S(1)}, u32[]{:S(2)}, u32[]{:S(2)}) collective-permute-start(bf16[2,336,128]{2,1,0:T(8,128)(2,1)S(1)} %pad_maximum_fusion.1.comp_a), channel_id=1, source_target_pairs={{0,32},{16,48},{32,64},{48,80},{64,96},{80,112},{96,0},{112,16},{1... | collective-permute-start | bytes 516104 | tf_op jit(solution)/shard_map/ppermute | solution.py:467
  35.5 25.7 %collective-permute-start.18 = (bf16[128,4096]{1,0:T(8,128)(2,1)}, bf16[128,4096]{1,0:T(8,128)(2,1)S(1)}, u32[]{:S(2)}, u32[]{:S(2)}) collective-permute-start(bf16[128,4096]{1,0:T(8,128)(2,1)} %bitcast.74), channel_id=1, source_target_pairs={{0,2},{1,3},{2,4},{3,5},{4,6},{5,7},{6,0},{7,1},{8,10},{9,11},{10,... | collective-permute-start | bytes 3145736 | tf_op jit(solution)/shard_map/ppermute | solution.py:41
  40.9 34.6 %copy-start.28 = (bf16[2,336,128]{2,1,0:T(8,128)(2,1)}, bf16[2,336,128]{2,1,0:T(8,128)(2,1)S(1)}, u32[]{:S(2)}) copy-start(bf16[2,336,128]{2,1,0:T(8,128)(2,1)S(1)} %collective-permute-done.38.comp_b) | copy-start | bytes 516100
  40.9 5.4 %collective-permute-start.39 = (bf16[2,336,128]{2,1,0:T(8,128)(2,1)S(1)}, bf16[2,336,128]{2,1,0:T(8,128)(2,1)S(1)}, u32[]{:S(2)}, u32[]{:S(2)}) collective-permute-start(bf16[2,336,128]{2,1,0:T(8,128)(2,1)S(1)} %pad_maximum_fusion.1.comp_a), channel_id=1, source_target_pairs={{0,96},{16,112},{32,0},{48,16},{64,32},{80,48},{96,64},{112,80},{1... | collective-permute-start | bytes 516104 | tf_op jit(solution)/shard_map/ppermute | solution.py:467
  46.3 6.9 %collective-permute-start.40 = (bf16[2,336,128]{2,1,0:T(8,128)(2,1)S(1)}, bf16[2,336,128]{2,1,0:T(8,128)(2,1)S(1)}, u32[]{:S(2)}, u32[]{:S(2)}) collective-permute-start(bf16[2,336,128]{2,1,0:T(8,128)(2,1)S(1)} %pad_maximum_fusion.1.comp_a), channel_id=1, source_target_pairs={{0,64},{16,80},{32,96},{48,112},{64,0},{80,16},{96,32},{112,48},{1... | collective-permute-start | bytes 516104 | tf_op jit(solution)/shard_map/ppermute | solution.py:467
  53.3 22.3 %collective-permute-start.20 = (bf16[128,4096]{1,0:T(8,128)(2,1)}, bf16[128,4096]{1,0:T(8,128)(2,1)}, u32[]{:S(2)}, u32[]{:S(2)}) collective-permute-start(bf16[128,4096]{1,0:T(8,128)(2,1)} %bitcast.75), channel_id=1, source_target_pairs={{0,6},{1,7},{2,0},{3,1},{4,2},{5,3},{6,4},{7,5},{8,14},{9,15},{10,... | collective-permute-start | bytes 3145736 | tf_op jit(solution)/shard_map/ppermute | solution.py:45
  56.0 22.1 %collective-permute-start.24 = (bf16[128,4096]{1,0:T(8,128)(2,1)}, bf16[128,4096]{1,0:T(8,128)(2,1)}, u32[]{:S(2)}, u32[]{:S(2)}) collective-permute-start(bf16[128,4096]{1,0:T(8,128)(2,1)} %bitcast.76), channel_id=1, source_target_pairs={{0,8},{1,9},{2,10},{3,11},{4,12},{5,13},{6,14},{7,15},{8,0},{9,1},... | collective-permute-start | bytes 3145736 | tf_op jit(solution)/shard_map/ppermute | solution.py:49
  56.0 20.7 %collective-permute-start.7 = (bf16[112,4096]{1,0:T(8,128)(2,1)S(1)}, bf16[112,4096]{1,0:T(8,128)(2,1)S(1)}, u32[]{:S(2)}, u32[]{:S(2)}) collective-permute-start(bf16[112,4096]{1,0:T(8,128)(2,1)S(1)} %get-tuple-element.42), channel_id=1, source_target_pairs={{0,24},{1,25},{2,26},{3,27},{4,28},{5,29},{6,30},{7,31},{8,16},{9,... | collective-permute-start | bytes 2752520 | tf_op jit(solution)/shard_map/ppermute | solution.py:494
  56.5 24.1 %collective-permute-start.33 = (bf16[128,4096]{1,0:T(8,128)(2,1)}, bf16[128,4096]{1,0:T(8,128)(2,1)S(1)}, u32[]{:S(2)}, u32[]{:S(2)}) collective-permute-start(bf16[128,4096]{1,0:T(8,128)(2,1)} %bitcast.77), channel_id=1, source_target_pairs={{0,1},{1,0},{2,3},{3,2},{4,5},{5,4},{6,7},{7,6},{8,9},{9,8},{10,11... | collective-permute-start | bytes 3145736 | tf_op jit(solution)/shard_map/ppermute | solution.py:53
  61.2 84.5 %copy-start.5 = (bf16[128,4096]{1,0:T(8,128)(2,1)}, bf16[128,4096]{1,0:T(8,128)(2,1)S(1)}, u32[]{:S(2)}) copy-start(bf16[128,4096]{1,0:T(8,128)(2,1)S(1)} %collective-permute-done.18.refs_4_) | copy-start | bytes 3145732
  61.2 84.5 %collective-permute-start.3 = (bf16[448,4096]{1,0:T(8,128)(2,1)}, bf16[448,4096]{1,0:T(8,128)(2,1)}, u32[]{:S(2)}, u32[]{:S(2)}) collective-permute-start(bf16[448,4096]{1,0:T(8,128)(2,1)} %wv.1), channel_id=1, source_target_pairs={{0,1},{1,0},{2,3},{3,2},{4,5},{5,4},{6,7},{7,6},{8,9},{9,8},{10,11... | collective-permute-start | bytes 11010056 | tf_op jit(solution)/shard_map/ppermute | solution.py:53
  75.6 20.3 %collective-permute-start.2 = (bf16[448,1024]{1,0:T(8,128)(2,1)}, bf16[448,1024]{1,0:T(8,128)(2,1)S(1)}, u32[]{:S(2)}, u32[]{:S(2)}) collective-permute-start(bf16[448,1024]{1,0:T(8,128)(2,1)} %collective-permute-done.1.refs_2_), channel_id=1, source_target_pairs={{0,1},{1,0},{2,3},{3,2},{4,5},{5,4},{6,7},{7,6},{8,9},{9,8},{10,11... | collective-permute-start | bytes 2752520 | tf_op jit(solution)/shard_map/ppermute | solution.py:53
  76.7 53.7 %copy-start.13 = (bf16[112,4096]{1,0:T(8,128)(2,1)}, bf16[112,4096]{1,0:T(8,128)(2,1)S(1)}, u32[]{:S(2)}) copy-start(bf16[112,4096]{1,0:T(8,128)(2,1)S(1)} %collective-permute-done.7.refs_9_) | copy-start | bytes 2752516
  76.7 16.4 %collective-permute-start.19 = (bf16[64,4096]{1,0:T(8,128)(2,1)S(1)}, bf16[64,4096]{1,0:T(8,128)(2,1)S(1)}, u32[]{:S(2)}, u32[]{:S(2)}) collective-permute-start(bf16[64,4096]{1,0:T(8,128)(2,1)S(1)} %slice.18), channel_id=1, source_target_pairs={{0,2},{1,3},{2,4},{3,5},{4,6},{5,7},{6,0},{7,1},{8,10},{9,11},{10,... | collective-permute-start | bytes 1572872 | tf_op jit(solution)/shard_map/ppermute | solution.py:41
  78.1 17.8 %collective-permute-start.21 = (bf16[64,4096]{1,0:T(8,128)(2,1)S(1)}, bf16[64,4096]{1,0:T(8,128)(2,1)}, u32[]{:S(2)}, u32[]{:S(2)}) collective-permute-start(bf16[64,4096]{1,0:T(8,128)(2,1)S(1)} %slice.19), channel_id=1, source_target_pairs={{0,6},{1,7},{2,0},{3,1},{4,2},{5,3},{6,4},{7,5},{8,14},{9,15},{10,... | collective-permute-start | bytes 1572872 | tf_op jit(solution)/shard_map/ppermute | solution.py:45
  80.7 65.0 %copy-start.10 = (bf16[128,4096]{1,0:T(8,128)(2,1)}, bf16[128,4096]{1,0:T(8,128)(2,1)S(1)}, u32[]{:S(2)}) copy-start(bf16[128,4096]{1,0:T(8,128)(2,1)S(1)} %collective-permute-done.33.refs_1_) | copy-start | bytes 3145732
  80.7 23.9 %collective-permute-start.5 = (bf16[112,4096]{1,0:T(8,128)(2,1)}, bf16[112,4096]{1,0:T(8,128)(2,1)S(1)}, u32[]{:S(2)}, u32[]{:S(2)}) collective-permute-start(bf16[112,4096]{1,0:T(8,128)(2,1)} %collective-permute-done.4.refs_6_), channel_id=1, source_target_pairs={{0,32},{16,48},{32,64},{48,80},{64,96},{80,112},{96,0},{112,16},{1... | collective-permute-start | bytes 2752520 | tf_op jit(solution)/shard_map/ppermute | solution.py:525
  93.2 37.9 %copy-start.21 = (bf16[64,4096]{1,0:T(8,128)(2,1)}, bf16[64,4096]{1,0:T(8,128)(2,1)S(1)}, u32[]{:S(2)}) copy-start(bf16[64,4096]{1,0:T(8,128)(2,1)S(1)} %collective-permute-done.19.refs_0_) | copy-start | bytes 1572868
  93.2 22.7 %collective-permute-start.6 = (bf16[112,4096]{1,0:T(8,128)(2,1)}, bf16[112,4096]{1,0:T(8,128)(2,1)S(1)}, u32[]{:S(2)}, u32[]{:S(2)}) collective-permute-start(bf16[112,4096]{1,0:T(8,128)(2,1)} %collective-permute-done.4.refs_6_), channel_id=1, source_target_pairs={{0,96},{16,112},{32,0},{48,16},{64,32},{80,48},{96,64},{112,80},{1... | collective-permute-start | bytes 2752520 | tf_op jit(solution)/shard_map/ppermute | solution.py:526
  95.9 20.0 %collective-permute-start.8 = (bf16[112,4096]{1,0:T(8,128)(2,1)}, bf16[112,4096]{1,0:T(8,128)(2,1)S(1)}, u32[]{:S(2)}, u32[]{:S(2)}) collective-permute-start(bf16[112,4096]{1,0:T(8,128)(2,1)} %collective-permute-done.4.refs_6_), channel_id=1, source_target_pairs={{0,1},{1,0},{2,3},{3,2},{4,5},{5,4},{6,7},{7,6},{8,9},{9,8},{10,11... | collective-permute-start | bytes 2752520 | tf_op jit(solution)/shard_map/ppermute | solution.py:53
  95.9 34.6 %copy-start.14 = (bf16[448,1024]{1,0:T(8,128)(2,1)}, bf16[448,1024]{1,0:T(8,128)(2,1)S(1)}, u32[]{:S(2)}) copy-start(bf16[448,1024]{1,0:T(8,128)(2,1)S(1)} %collective-permute-done.2.refs_3_) | copy-start | bytes 2752516
  95.9 20.5 %collective-permute-start.11 = (bf16[112,4096]{1,0:T(8,128)(2,1)S(1)}, bf16[112,4096]{1,0:T(8,128)(2,1)S(1)}, u32[]{:S(2)}, u32[]{:S(2)}) collective-permute-start(bf16[112,4096]{1,0:T(8,128)(2,1)S(1)} %collective-permute-done.7.refs_9_), channel_id=1, source_target_pairs={{0,1},{1,0},{2,3},{3,2},{4,5},{5,4},{6,7},{7,6},{8,9},{9,8},{10,11... | collective-permute-start | bytes 2752520 | tf_op jit(solution)/shard_map/ppermute | solution.py:53
  104.6 25.8 %collective-permute-start.25 = (bf16[128,4096]{1,0:T(8,128)(2,1)}, bf16[128,4096]{1,0:T(8,128)(2,1)S(1)}, u32[]{:S(2)}, u32[]{:S(2)}) collective-permute-start(bf16[128,4096]{1,0:T(8,128)(2,1)} %collective-permute-done.24.refs_2_), channel_id=1, source_target_pairs={{0,2},{1,3},{2,4},{3,5},{4,6},{5,7},{6,0},{7,1},{8,10},{9,11},{10,... | collective-permute-start | bytes 3145736 | tf_op jit(solution)/shard_map/ppermute | solution.py:41
  115.9 14.6 %collective-permute-start.9 = (bf16[112,4096]{1,0:T(8,128)(2,1)S(1)}, bf16[112,4096]{1,0:T(8,128)(2,1)S(1)}, u32[]{:S(2)}, u32[]{:S(2)}) collective-permute-start(bf16[112,4096]{1,0:T(8,128)(2,1)S(1)} %collective-permute-done.5.refs_7_), channel_id=1, source_target_pairs={{0,1},{1,0},{2,3},{3,2},{4,5},{5,4},{6,7},{7,6},{8,9},{9,8},{10,11... | collective-permute-start | bytes 2752520 | tf_op jit(solution)/shard_map/ppermute | solution.py:53
  115.9 15.2 %collective-permute-start.10 = (bf16[112,4096]{1,0:T(8,128)(2,1)S(1)}, bf16[112,4096]{1,0:T(8,128)(2,1)S(1)}, u32[]{:S(2)}, u32[]{:S(2)}) collective-permute-start(bf16[112,4096]{1,0:T(8,128)(2,1)S(1)} %collective-permute-done.6.refs_8_), channel_id=1, source_target_pairs={{0,1},{1,0},{2,3},{3,2},{4,5},{5,4},{6,7},{7,6},{8,9},{9,8},{10,11... | collective-permute-start | bytes 2752520 | tf_op jit(solution)/shard_map/ppermute | solution.py:53
  116.4 4.0 %collective-permute-start.22 = (bf16[64,4096]{1,0:T(8,128)(2,1)S(1)}, bf16[64,4096]{1,0:T(8,128)(2,1)S(1)}, u32[]{:S(2)}, u32[]{:S(2)}) collective-permute-start(bf16[64,4096]{1,0:T(8,128)(2,1)S(1)} %collective-permute-done.19.refs_0_), channel_id=1, source_target_pairs={{0,1},{1,0},{2,3},{3,2},{4,5},{5,4},{6,7},{7,6},{8,9},{9,8},{10,11... | collective-permute-start | bytes 1572872 | tf_op jit(solution)/shard_map/ppermute | solution.py:53
  120.4 40.1 %collective-permute-start.27 = (bf16[128,4096]{1,0:T(8,128)(2,1)}, bf16[128,4096]{1,0:T(8,128)(2,1)}, u32[]{:S(2)}, u32[]{:S(2)}) collective-permute-start(bf16[128,4096]{1,0:T(8,128)(2,1)} %collective-permute-done.24.refs_2_), channel_id=1, source_target_pairs={{0,6},{1,7},{2,0},{3,1},{4,2},{5,3},{6,4},{7,5},{8,14},{9,15},{10,... | collective-permute-start | bytes 3145736 | tf_op jit(solution)/shard_map/ppermute | solution.py:45
  130.4 32.2 %collective-permute-start.34 = (bf16[128,4096]{1,0:T(8,128)(2,1)}, bf16[128,4096]{1,0:T(8,128)(2,1)}, u32[]{:S(2)}, u32[]{:S(2)}) collective-permute-start(bf16[128,4096]{1,0:T(8,128)(2,1)} %collective-permute-done.24.refs_2_), channel_id=1, source_target_pairs={{0,1},{1,0},{2,3},{3,2},{4,5},{5,4},{6,7},{7,6},{8,9},{9,8},{10,11... | collective-permute-start | bytes 3145736 | tf_op jit(solution)/shard_map/ppermute | solution.py:53
  130.5 32.7 %collective-permute-start.35 = (bf16[128,4096]{1,0:T(8,128)(2,1)S(1)}, bf16[128,4096]{1,0:T(8,128)(2,1)}, u32[]{:S(2)}, u32[]{:S(2)}) collective-permute-start(bf16[128,4096]{1,0:T(8,128)(2,1)S(1)} %collective-permute-done.18.refs_4_), channel_id=1, source_target_pairs={{0,1},{1,0},{2,3},{3,2},{4,5},{5,4},{6,7},{7,6},{8,9},{9,8},{10,11... | collective-permute-start | bytes 3145736 | tf_op jit(solution)/shard_map/ppermute | solution.py:53
  132.4 30.8 %collective-permute-start.36 = (bf16[128,4096]{1,0:T(8,128)(2,1)}, bf16[128,4096]{1,0:T(8,128)(2,1)}, u32[]{:S(2)}, u32[]{:S(2)}) collective-permute-start(bf16[128,4096]{1,0:T(8,128)(2,1)} %collective-permute-done.20.refs_6_), channel_id=1, source_target_pairs={{0,1},{1,0},{2,3},{3,2},{4,5},{5,4},{6,7},{7,6},{8,9},{9,8},{10,11... | collective-permute-start | bytes 3145736 | tf_op jit(solution)/shard_map/ppermute | solution.py:53
  145.7 16.9 %collective-permute-start.29 = (bf16[64,4096]{1,0:T(8,128)(2,1)}, bf16[64,4096]{1,0:T(8,128)(2,1)}, u32[]{:S(2)}, u32[]{:S(2)}) collective-permute-start(bf16[64,4096]{1,0:T(8,128)(2,1)} %copy-done.21), channel_id=1, source_target_pairs={{0,8},{1,9},{2,10},{3,11},{4,12},{5,13},{6,14},{7,15},{8,0},{9,1},... | collective-permute-start | bytes 1572872 | tf_op jit(solution)/shard_map/ppermute | solution.py:49
  160.5 19.4 %collective-permute-start.30 = (bf16[64,4096]{1,0:T(8,128)(2,1)}, bf16[64,4096]{1,0:T(8,128)(2,1)}, u32[]{:S(2)}, u32[]{:S(2)}) collective-permute-start(bf16[64,4096]{1,0:T(8,128)(2,1)} %collective-permute-done.21.refs_1_), channel_id=1, source_target_pairs={{0,8},{1,9},{2,10},{3,11},{4,12},{5,13},{6,14},{7,15},{8,0},{9,1},... | collective-permute-start | bytes 1572872 | tf_op jit(solution)/shard_map/ppermute | solution.py:49
  162.6 21.7 %collective-permute-start.26 = (bf16[128,4096]{1,0:T(8,128)(2,1)S(1)}, bf16[128,4096]{1,0:T(8,128)(2,1)S(1)}, u32[]{:S(2)}, u32[]{:S(2)}) collective-permute-start(bf16[128,4096]{1,0:T(8,128)(2,1)S(1)} %collective-permute-done.25.refs_4_), channel_id=1, source_target_pairs={{0,1},{1,0},{2,3},{3,2},{4,5},{5,4},{6,7},{7,6},{8,9},{9,8},{10,11... | collective-permute-start | bytes 3145736 | tf_op jit(solution)/shard_map/ppermute | solution.py:53
  162.6 25.1 %collective-permute-start.28 = (bf16[128,4096]{1,0:T(8,128)(2,1)}, bf16[128,4096]{1,0:T(8,128)(2,1)S(1)}, u32[]{:S(2)}, u32[]{:S(2)}) collective-permute-start(bf16[128,4096]{1,0:T(8,128)(2,1)} %collective-permute-done.27.refs_6_), channel_id=1, source_target_pairs={{0,1},{1,0},{2,3},{3,2},{4,5},{5,4},{6,7},{7,6},{8,9},{9,8},{10,11... | collective-permute-start | bytes 3145736 | tf_op jit(solution)/shard_map/ppermute | solution.py:53
  163.1 16.9 %collective-permute-start.13 = (bf16[128,2048]{1,0:T(8,128)(2,1)}, bf16[128,2048]{1,0:T(8,128)(2,1)S(1)}, u32[]{:S(2)}, u32[]{:S(2)}) collective-permute-start(bf16[128,2048]{1,0:T(8,128)(2,1)} %get-tuple-element.29), channel_id=1, source_target_pairs={{0,2},{1,3},{2,4},{3,5},{4,6},{5,7},{6,0},{7,1},{8,10},{9,11},{10,... | collective-permute-start | bytes 1572872 | tf_op jit(solution)/shard_map/ppermute | solution.py:41
  163.1 17.3 %collective-permute-start.16 = (bf16[128,2048]{1,0:T(8,128)(2,1)}, bf16[128,2048]{1,0:T(8,128)(2,1)S(1)}, u32[]{:S(2)}, u32[]{:S(2)}) collective-permute-start(bf16[128,2048]{1,0:T(8,128)(2,1)} %get-tuple-element.33), channel_id=1, source_target_pairs={{0,6},{1,7},{2,0},{3,1},{4,2},{5,3},{6,4},{7,5},{8,14},{9,15},{10,... | collective-permute-start | bytes 1572872 | tf_op jit(solution)/shard_map/ppermute | solution.py:45
  179.9 2.2 %collective-permute-start.23 = (bf16[64,4096]{1,0:T(8,128)(2,1)}, bf16[64,4096]{1,0:T(8,128)(2,1)S(1)}, u32[]{:S(2)}, u32[]{:S(2)}) collective-permute-start(bf16[64,4096]{1,0:T(8,128)(2,1)} %collective-permute-done.21.refs_1_), channel_id=1, source_target_pairs={{0,1},{1,0},{2,3},{3,2},{4,5},{5,4},{6,7},{7,6},{8,9},{9,8},{10,11... | collective-permute-start | bytes 1572872 | tf_op jit(solution)/shard_map/ppermute | solution.py:53
  180.0 2.8 %collective-permute-start.31 = (bf16[64,4096]{1,0:T(8,128)(2,1)}, bf16[64,4096]{1,0:T(8,128)(2,1)S(1)}, u32[]{:S(2)}, u32[]{:S(2)}) collective-permute-start(bf16[64,4096]{1,0:T(8,128)(2,1)} %collective-permute-done.29.refs_8_), channel_id=1, source_target_pairs={{0,1},{1,0},{2,3},{3,2},{4,5},{5,4},{6,7},{7,6},{8,9},{9,8},{10,11... | collective-permute-start | bytes 1572872 | tf_op jit(solution)/shard_map/ppermute | solution.py:53
  180.5 3.7 %collective-permute-start.32 = (bf16[64,4096]{1,0:T(8,128)(2,1)}, bf16[64,4096]{1,0:T(8,128)(2,1)S(1)}, u32[]{:S(2)}, u32[]{:S(2)}) collective-permute-start(bf16[64,4096]{1,0:T(8,128)(2,1)} %collective-permute-done.30.refs_9_), channel_id=1, source_target_pairs={{0,1},{1,0},{2,3},{3,2},{4,5},{5,4},{6,7},{7,6},{8,9},{9,8},{10,11... | collective-permute-start | bytes 1572872 | tf_op jit(solution)/shard_map/ppermute | solution.py:53
  182.1 22.0 %collective-permute-start.12 = (bf16[128,2048]{1,0:T(8,128)(2,1)S(1)}, bf16[128,2048]{1,0:T(8,128)(2,1)S(1)}, u32[]{:S(2)}, u32[]{:S(2)}) collective-permute-start(bf16[128,2048]{1,0:T(8,128)(2,1)S(1)} %copy-done.24), channel_id=1, source_target_pairs={{0,6},{1,7},{2,0},{3,1},{4,2},{5,3},{6,4},{7,5},{8,14},{9,15},{10,... | collective-permute-start | bytes 1572872 | tf_op jit(solution)/shard_map/ppermute | solution.py:45
  182.8 21.3 %collective-permute-start.15 = (bf16[128,2048]{1,0:T(8,128)(2,1)S(1)}, bf16[128,2048]{1,0:T(8,128)(2,1)S(1)}, u32[]{:S(2)}, u32[]{:S(2)}) collective-permute-start(bf16[128,2048]{1,0:T(8,128)(2,1)S(1)} %copy-done.23), channel_id=1, source_target_pairs={{0,2},{1,3},{2,4},{3,5},{4,6},{5,7},{6,0},{7,1},{8,10},{9,11},{10,... | collective-permute-start | bytes 1572872 | tf_op jit(solution)/shard_map/ppermute | solution.py:41
  184.2 25.1 %collective-permute-start.14 = (bf16[128,2048]{1,0:T(8,128)(2,1)S(1)}, bf16[128,2048]{1,0:T(8,128)(2,1)S(1)}, u32[]{:S(2)}, u32[]{:S(2)}) collective-permute-start(bf16[128,2048]{1,0:T(8,128)(2,1)S(1)} %add_convert_fusion.3), channel_id=1, source_target_pairs={{0,2},{1,3},{2,4},{3,5},{4,6},{5,7},{6,0},{7,1},{8,10},{9,11},{10,... | collective-permute-start | bytes 1572872 | tf_op jit(solution)/shard_map/ppermute | solution.py:41
  184.3 25.0 %collective-permute-start.17 = (bf16[128,2048]{1,0:T(8,128)(2,1)S(1)}, bf16[128,2048]{1,0:T(8,128)(2,1)S(1)}, u32[]{:S(2)}, u32[]{:S(2)}) collective-permute-start(bf16[128,2048]{1,0:T(8,128)(2,1)S(1)} %add_convert_fusion.1), channel_id=1, source_target_pairs={{0,6},{1,7},{2,0},{3,1},{4,2},{5,3},{6,4},{7,5},{8,14},{9,15},{10,... | collective-permute-start | bytes 1572872 | tf_op jit(solution)/shard_map/ppermute | solution.py:45
  (24 other events, 299.4 us)
where the time goes:
time: 212 us; the launch traced here: 211 us
  waiting for transfers between devices  103 us (49%)
  Pallas kernels  60.2 us (28%)
  starting transfers between devices  38.3 us (18%)
  local copies, waits for them, and re-layouts  5.84 us (3%)
  other arithmetic  2.21 us (1%)
    ppermute x6, waiting for transfers between devices, right(): return lax.ppermute(v, 'tp', TO_RIGHT)  30.3 us
    pallas_call x2, Pallas kernels, grads(): pl.pallas_call(functools.partial(grads_kernel, first, base, count), grid_...  28.8 us
    ppermute x1, waiting for transfers between devices, everyones_components(): pair = jnp.stack([mine, lax.ppermute(mine, 'rep', TO_HI)])  20.7 us
    pallas_call x1, Pallas kernels, forward(): pl.pallas_call(functools.partial(forward_kernel, len(weights)), grid_spec...  14.7 us
    ppermute x6, waiting for transfers between devices, left(): return lax.ppermute(v, 'tp', TO_LEFT)  14.4 us
    ppermute x6, starting transfers between devices, left(): return lax.ppermute(v, 'tp', TO_LEFT)  13.7 us
    pallas_call x1, Pallas kernels, decode(): pl.pallas_call(decode_kernel, grid=(rows,), in_specs=[*[whole(v) for v in...  12.9 us
    ppermute x3, waiting for transfers between devices, everyones_components(): lax.ppermute(pair, 'rep', to)  12.6 us
  transfers between devices with their start and end apart: 41, of which 14 were waited for; matrix products, arithmetic and copies ran while one was open for 2% of the time, Pallas kernels for 27%

commit v1 on v0

--- a/solution.py
+++ b/solution.py
@@ -375,9 +375,10 @@
     return parts[:4], parts[4:]
 
 
-def decode_kernel(comp_a, comp_b, comp_c, comp_d, wv, cos_ref, ct_ref, upv, newv, cb_ref, fields, co4, mid):
+def decode_kernel(base, comp_a, comp_b, comp_c, comp_d, wv, cos_ref, ct_ref, *refs):
+    upv, newv, cb_ref, fields, co4, mid = refs[-6:]
     bf, f32 = jnp.bfloat16, jnp.float32
-    a = pl.program_id(0)
+    a = pl.program_id(0) + base
     comps = [ref.at[n] for ref in (comp_a, comp_b, comp_c, comp_d) for n in range(ref.shape[0])]
     replicas = len(comps)
     per = 128 // TOPK
@@ -385,7 +386,7 @@
     rows = fields.shape[1] // 3
     count = replicas * TOPK
 
-    @pl.when(a == 0)
+    @pl.when(a == base)
     def _():
         cb_ref[...] = jnp.zeros_like(cb_ref)
         for bl in range(per):
@@ -427,7 +428,7 @@
         newv[:, cols] = (wv[:, cols].astype(f32) - LEARN_RATE * update.astype(f32)).astype(bf)
 
 
-def decode(comp, w):
+def decode(base, end, comp, w, before=()):
     replicas = sum(v.shape[0] for v in comp)
     width = w.shape[1]
     rows = w.shape[0] // SPAN
@@ -437,13 +438,15 @@
     cb = jnp.asarray(cos, jnp.bfloat16)
     ct = jnp.asarray(cos.T / replicas, jnp.bfloat16)
     whole = lambda v: pl.BlockSpec(v.shape, lambda a: (0,) * v.ndim)
-    wide = pl.BlockSpec((SPAN, width), lambda a: (a, 0))
+    wide = pl.BlockSpec((SPAN, width), lambda a: (a + base, 0))
+    any_spec = pl.BlockSpec(memory_space=pl.ANY)
     out = jax.ShapeDtypeStruct(w.shape, jnp.bfloat16)
     bf = jnp.bfloat16
     return pl.pallas_call(
-        decode_kernel,
-        grid=(rows,),
-        in_specs=[*[whole(v) for v in comp], wide, whole(cb), whole(ct)],
+        functools.partial(decode_kernel, base),
+        grid=(end - base,),
+        in_specs=[*[whole(v) for v in comp], wide, whole(cb), whole(ct)] + [any_spec] * len(before),
+        input_output_aliases={len(comp) + 3 + n: n for n in range(len(before))},
         out_specs=[wide, wide],
         out_shape=[out, out],
         scratch_shapes=[
@@ -453,8 +456,7 @@
             pltpu.VMEM((groups * SPAN, per * SPAN), bf),
         ],
         cost_estimate=pl.CostEstimate(flops=8 << 30, bytes_accessed=12 << 20, transcendentals=0),
-        name="decode",
-    )(*comp, w, cb, ct)
+    )(*comp, w, cb, ct, *before)
 
 
 def everyones_components(comp_index, comp_value):
@@ -499,7 +501,10 @@
     hs_p = swap(hid_own)
     hz_p = swap(hz)
 
-    update, updated = decode(comp, w)
+    span_rows = w.shape[0] // SPAN
+    early = 2
+    update, updated = decode(0, early, comp, w)
+    update, updated = decode(early, span_rows, comp, w, (update, updated))
 
     half_rows = TOK // 2
     cut_a = from_l[:half_rows]

time: 212 us -> 186 us (0.88)
  waiting for transfers between devices: 103 us -> 76.8 us
  Pallas kernels: 60.2 us -> 63.8 us
    ppermute x1, waiting for transfers between devices: 20.7 us -> 0.01 us  [everyones_components(): pair = jnp.stack([mine, lax.ppermute(mine, 'rep', TO_HI)])]
    ppermute x6, waiting for transfers between devices: 14.4 us -> 5.88 us  [left(): return lax.ppermute(v, 'tp', TO_LEFT)]
    ppermute x1, waiting for transfers between devices: 0.01 us -> 8.46 us  [body(): lax.ppermute(lax.dynamic_slice_in_dim(w, far_q * quarter, quarter, 0), ('...]
    ppermute x1, waiting for transfers between devices: 0.01 us -> 6.3 us  [body(): lax.ppermute(lax.dynamic_slice_in_dim(w, y * quarter, quarter, 0), ('rep'...]
    ppermute x3, waiting for transfers between devices: 12.6 us -> 7.51 us  [everyones_components(): lax.ppermute(pair, 'rep', to)]
    ppermute x6, waiting for transfers between devices: 30.3 us -> 25.4 us  [right(): return lax.ppermute(v, 'tp', TO_RIGHT)]
    ppermute x17, waiting for transfers between devices: 5.79 us -> 1.84 us  [swap(): return lax.ppermute(v, 'tp', TO_CORE)]
    pallas_call x1 -> x2, Pallas kernels: 12.9 us -> 16.4 us  [decode(): pl.pallas_call(functools.partial(decode_kernel, base), grid=(end - base,)...]
  transfers between devices with their start and end apart: 41 -> 41, of which waited for: 14 -> 14; matrix products, arithmetic and copies ran while one was open for 2% -> 1% of each run, Pallas kernels for 27% -> 34%
where the time goes in v1:
time: 186 us
  waiting for transfers between devices  76.8 us (41%)
  Pallas kernels  63.8 us (34%)
  starting transfers between devices  36.7 us (20%)
  local copies, waits for them, and re-layouts  3.75 us (2%)
  other arithmetic  3.7 us (2%)
    pallas_call x2, Pallas kernels, grads(): pl.pallas_call(functools.partial(grads_kernel, first, base, count), grid_...  28.7 us
    ppermute x6, waiting for transfers between devices, right(): return lax.ppermute(v, 'tp', TO_RIGHT)  25.4 us
    pallas_call x2, Pallas kernels, decode(): pl.pallas_call(functools.partial(decode_kernel, base), grid=(end - base,)...  16.4 us
    pallas_call x1, Pallas kernels, forward(): pl.pallas_call(functools.partial(forward_kernel, len(weights)), grid_spec...  14.8 us
    ppermute x6, starting transfers between devices, left(): return lax.ppermute(v, 'tp', TO_LEFT)  12 us
    ppermute x1, waiting for transfers between devices, body(): w_qm = lax.ppermute(w_q0, 'rep', TO_UP)  9.07 us
    ppermute x1, waiting for transfers between devices, body(): w_qp = lax.ppermute(w_q0, 'rep', TO_DOWN)  8.97 us
    ppermute x1, waiting for transfers between devices, body(): lax.ppermute(lax.dynamic_slice_in_dim(w, far_q * quarter, quarter, 0), ('...  8.46 us
  transfers between devices with their start and end apart: 41, of which 14 were waited for; matrix products, arithmetic and copies ran while one was open for 1% of the time, Pallas kernels for 34%

profile of v1, /device:TPU:0, one launch (start us, length us, event | category | flops | bytes accessed | tf_op | source)
XLA Modules:
  0.0 185.7 jit_solution(11763511318817010758)
XLA Ops:
  0.6 0.9 fusion.2
  1.5 0.8 pad_maximum_fusion.2
  2.4 4.1 %collective-permute-start.37 = (bf16[336,128]{1,0:T(8,128)(2,1)S(1)}, bf16[336,128]{1,0:T(8,128)(2,1)S(1)}, u32[]{:S(2)}, u32[]{:S(2)}) collective-permute-start(bf16[336,128]{1,0:T(8,128)(2,1)S(1)} %reshape.46), channel_id=1, source_target_pairs={{0,16},{16,0},{32,48},{48,32},{64,80},{80,64},{96,112},{112,96},{1... | collective-permute-start | bytes 258056 | tf_op jit(solution)/shard_map/ppermute | solution.py:468
  6.5 0.6 stack.81.spots.pos.idx
  7.1 3.9 %hidden_halves.1 = (bf16[448,1024]{1,0:T(8,128)(2,1)}, bf16[448,1024]{1,0:T(8,128)(2,1)}) custom-call(s32[18]{0:T(128)} %stack.81.spots.pos.idx, bf16[448,2048]{1,0:T(8,128)(2,1)} %bitcast.65, bf16[448,2048]{1,0:T(8,128)(2,1)} %bitcast.68), custom_call_target="tpu_custom_call" | custom-call | flops 9175040 | bytes 5505024 | tf_op jit(solution)/shard_map/hidden_halves/pallas_call | solution.py:98
  11.1 1.1 collective-permute-start.1
  12.3 1.6 collective-permute-start.38
  13.9 1.7 collective-permute-start.39
  15.6 1.6 constant_dynamic-slice_fusion
  17.6 2.4 %collective-permute-done.38.comp_b = bf16[2,336,128]{2,1,0:T(8,128)(2,1)S(1)} collective-permute-done((bf16[2,336,128]{2,1,0:T(8,128)(2,1)S(1)}, bf16[2,336,128]{2,1,0:T(8,128)(2,1)S(1)}, u32[]{:S(2)}, u32[]{:S(2)}) %collective-permute-start.38) | collective-permute-done | bytes 172064 | tf_op jit(solution)/shard_map/ppermute | solution.py:469
  20.1 1.5 collective-permute-start.18
  21.5 1.9 %collective-permute-start.40 = (bf16[2,336,128]{2,1,0:T(8,128)(2,1)S(1)}, bf16[2,336,128]{2,1,0:T(8,128)(2,1)}, u32[]{:S(2)}, u32[]{:S(2)}) collective-permute-start(bf16[2,336,128]{2,1,0:T(8,128)(2,1)S(1)} %pad_maximum_fusion.1.comp_a), channel_id=1, source_target_pairs={{0,64},{16,80},{32,96},{48,112},{64,0},{80,16},{96,32},{112,48},{1... | collective-permute-start | bytes 516104 | tf_op jit(solution)/shard_map/ppermute | solution.py:469
  23.5 5.1 %collective-permute-done.40.comp_d = bf16[2,336,128]{2,1,0:T(8,128)(2,1)} collective-permute-done((bf16[2,336,128]{2,1,0:T(8,128)(2,1)S(1)}, bf16[2,336,128]{2,1,0:T(8,128)(2,1)}, u32[]{:S(2)}, u32[]{:S(2)}) %collective-permute-start.40) | collective-permute-done | bytes 172064 | tf_op jit(solution)/shard_map/ppermute | solution.py:469
  28.6 1.7 collective-permute-start.20
  30.3 1.0 collective-permute-start.24
  31.3 3.4 %collective-permute-done.1.refs_2_ = bf16[448,1024]{1,0:T(8,128)(2,1)} collective-permute-done((bf16[448,1024]{1,0:T(8,128)(2,1)}, bf16[448,1024]{1,0:T(8,128)(2,1)}, u32[]{:S(2)}, u32[]{:S(2)}) %collective-permute-start.1) | collective-permute-done | bytes 917536 | tf_op jit(solution)/shard_map/ppermute | solution.py:49
  34.7 0.7 collective-permute-start.7
  35.4 6.3 %collective-permute-done.4.refs_6_ = bf16[112,4096]{1,0:T(8,128)(2,1)S(1)} collective-permute-done((bf16[112,4096]{1,0:T(8,128)(2,1)S(1)}, bf16[112,4096]{1,0:T(8,128)(2,1)S(1)}, u32[]{:S(2)}, u32[]{:S(2)}) %collective-permute-start.4) | collective-permute-done | bytes 917536 | tf_op jit(solution)/shard_map/ppermute | solution.py:494
  41.7 4.0 %collective-permute-done.18.refs_4_ = bf16[128,4096]{1,0:T(8,128)(2,1)S(1)} collective-permute-done((bf16[128,4096]{1,0:T(8,128)(2,1)S(1)}, bf16[128,4096]{1,0:T(8,128)(2,1)S(1)}, u32[]{:S(2)}, u32[]{:S(2)}) %collective-permute-start.18) | collective-permute-done | bytes 1048608 | tf_op jit(solution)/shard_map/ppermute | solution.py:41
  45.7 5.9 %collective-permute-done.20.refs_6_ = bf16[128,4096]{1,0:T(8,128)(2,1)S(1)} collective-permute-done((bf16[128,4096]{1,0:T(8,128)(2,1)S(1)}, bf16[128,4096]{1,0:T(8,128)(2,1)S(1)}, u32[]{:S(2)}, u32[]{:S(2)}) %collective-permute-start.20) | collective-permute-done | bytes 1048608 | tf_op jit(solution)/shard_map/ppermute | solution.py:45
  51.6 8.5 %collective-permute-done.7.refs_9_ = bf16[112,4096]{1,0:T(8,128)(2,1)S(1)} collective-permute-done((bf16[112,4096]{1,0:T(8,128)(2,1)S(1)}, bf16[112,4096]{1,0:T(8,128)(2,1)S(1)}, u32[]{:S(2)}, u32[]{:S(2)}) %collective-permute-start.7) | collective-permute-done | bytes 917536 | tf_op jit(solution)/shard_map/ppermute | solution.py:496
  60.1 1.5 collective-permute-start.19
  61.6 1.7 collective-permute-start.21
  63.6 10.5 %collective-permute-done.19.refs_0_ = bf16[64,4096]{1,0:T(8,128)(2,1)} collective-permute-done((bf16[64,4096]{1,0:T(8,128)(2,1)S(1)}, bf16[64,4096]{1,0:T(8,128)(2,1)}, u32[]{:S(2)}, u32[]{:S(2)}) %collective-permute-start.19) | collective-permute-done | bytes 524320 | tf_op jit(solution)/shard_map/ppermute | solution.py:41
  74.1 1.5 collective-permute-start.6
  75.7 0.5 collective-permute-start.11
  76.2 9.1 %collective-permute-done.5.refs_7_ = bf16[112,4096]{1,0:T(8,128)(2,1)} collective-permute-done((bf16[112,4096]{1,0:T(8,128)(2,1)S(1)}, bf16[112,4096]{1,0:T(8,128)(2,1)}, u32[]{:S(2)}, u32[]{:S(2)}) %collective-permute-start.5) | collective-permute-done | bytes 917536 | tf_op jit(solution)/shard_map/ppermute | solution.py:530
  85.5 9.0 %collective-permute-done.6.refs_8_ = bf16[112,4096]{1,0:T(8,128)(2,1)} collective-permute-done((bf16[112,4096]{1,0:T(8,128)(2,1)S(1)}, bf16[112,4096]{1,0:T(8,128)(2,1)}, u32[]{:S(2)}, u32[]{:S(2)}) %collective-permute-start.6) | collective-permute-done | bytes 917536 | tf_op jit(solution)/shard_map/ppermute | solution.py:531
  94.5 0.6 collective-permute-start.10
  95.4 0.9 copy-done.15
  96.3 0.5 collective-permute-start.22
  96.9 6.2 %shard_map.154 = (bf16[448,4096]{1,0:T(8,128)(2,1)}, bf16[448,4096]{1,0:T(8,128)(2,1)}) custom-call(bf16[2,336,128]{2,1,0:T(8,128)(2,1)} %copy-done.7, bf16[2,336,128]{2,1,0:T(8,128)(2,1)} %copy-done.23, bf16[2,336,128]{2,1,0:T(8,128)(2,1)} %copy-done.24, bf16[2,336,128]{2,1,0:T(8,128)(2,1)} %collective-permute-done.40.comp_d, bf16[448,4096]{1,0:T(8,128)(2,1)} %wv.3, ...), custom_call_target="tpu_custom_call" | custom-call | flops 8589934592 | bytes 12582912 | tf_op jit(solution)/shard_map/pallas_call | solution.py:445
  103.1 1.6 collective-permute-start.27
  104.7 4.5 %collective-permute-done.25.refs_4_ = bf16[128,4096]{1,0:T(8,128)(2,1)S(1)} collective-permute-done((bf16[128,4096]{1,0:T(8,128)(2,1)}, bf16[128,4096]{1,0:T(8,128)(2,1)S(1)}, u32[]{:S(2)}, u32[]{:S(2)}) %collective-permute-start.25) | collective-permute-done | bytes 1048608 | tf_op jit(solution)/shard_map/ppermute | solution.py:41
  109.2 0.5 collective-permute-start.35
  109.8 10.2 %shard_map.155 = (bf16[448,4096]{1,0:T(8,128)(2,1)}, bf16[448,4096]{1,0:T(8,128)(2,1)}) custom-call(bf16[2,336,128]{2,1,0:T(8,128)(2,1)} %copy-done.7, bf16[2,336,128]{2,1,0:T(8,128)(2,1)} %copy-done.23, bf16[2,336,128]{2,1,0:T(8,128)(2,1)} %copy-done.24, ...), custom_call_target="tpu_custom_call", output_to_operand_aliasing={{0}: (7, {}), {1}: (8, {})} | custom-call | flops 8589934592 | bytes 12582912 | tf_op jit(solution)/shard_map/pallas_call | solution.py:445
  120.1 14.8 %forward.1 = (bf16[128,2048]{1,0:T(8,128)(2,1)}, bf16[128,2048]{1,0:T(8,128)(2,1)}, bf16[128,2048]{1,0:T(8,128)(2,1)}, bf16[128,2048]{1,0:T(8,128)(2,1)}, bf16[1...) custom-call(s32[18]{0:T(128)} %stack.81.spots.pos.idx, ...), custom_call_target="tpu_custom_call" | custom-call | flops 7516192768 | bytes 23068672 | tf_op jit(solution)/shard_map/forward/pallas_call | solution.py:353
  134.9 2.1 %collective-permute-start.30 = (bf16[64,4096]{1,0:T(8,128)(2,1)}, bf16[64,4096]{1,0:T(8,128)(2,1)S(1)}, u32[]{:S(2)}, u32[]{:S(2)}) collective-permute-start(bf16[64,4096]{1,0:T(8,128)(2,1)} %collective-permute-done.21.refs_1_), channel_id=1, source_target_pairs={{0,8},{1,9},{2,10},{3,11},{4,12},{5,13},{6,14},{7,15},{8,0},{9,1},... | collective-permute-start | bytes 1572872 | tf_op jit(solution)/shard_map/ppermute | solution.py:49
  137.7 3.5 %collective-permute-start.16 = (bf16[128,2048]{1,0:T(8,128)(2,1)}, bf16[128,2048]{1,0:T(8,128)(2,1)S(1)}, u32[]{:S(2)}, u32[]{:S(2)}) collective-permute-start(bf16[128,2048]{1,0:T(8,128)(2,1)} %get-tuple-element.35), channel_id=1, source_target_pairs={{0,6},{1,7},{2,0},{3,1},{4,2},{5,3},{6,4},{7,5},{8,14},{9,15},{10,... | collective-permute-start | bytes 1572872 | tf_op jit(solution)/shard_map/ppermute | solution.py:45
  141.2 13.4 %grads_first.1 = (bf16[448,4096]{1,0:T(8,128)(2,1)}, bf16[448,2048]{1,0:T(8,128)(2,1)}, bf16[448,2048]{1,0:T(8,128)(2,1)}) custom-call(s32[18]{0:T(128)} %stack.81.spots.pos.idx, bf16[128,4096]{1,0:T(8,128)(2,1)} %bitcast.74, bf16[128,4096]{1,0:T(8,128)(2,1)} %copy-done.10, bf16[128,4096]{1,0:T(8,128)(2,1)} %collective-permute-done.24.refs_2_, ...), custom_call_target="tpu_custom_call" | custom-call | flops 7516192768 | bytes 25165824 | tf_op jit(solution)/shard_map/grads_first/pallas_call | solution.py:263
  155.6 1.2 collective-permute-done.23.refs_3_
  157.0 0.6 collective-permute-done.31.refs_10_
  157.6 1.3 collective-permute-start.15
  159.0 3.2 %collective-permute-start.17 = (bf16[128,2048]{1,0:T(8,128)(2,1)S(1)}, bf16[128,2048]{1,0:T(8,128)(2,1)S(1)}, u32[]{:S(2)}, u32[]{:S(2)}) collective-permute-start(bf16[128,2048]{1,0:T(8,128)(2,1)S(1)} %add_convert_fusion.1), channel_id=1, source_target_pairs={{0,6},{1,7},{2,0},{3,1},{4,2},{5,3},{6,4},{7,5},{8,14},{9,15},{10,... | collective-permute-start | bytes 1572872 | tf_op jit(solution)/shard_map/ppermute | solution.py:45
  162.3 15.3 %grads_second.1 = (bf16[448,4096]{1,0:T(8,128)(2,1)}, bf16[448,2048]{1,0:T(8,128)(2,1)}, bf16[448,2048]{1,0:T(8,128)(2,1)}) custom-call(s32[18]{0:T(128)} %stack.81.spots.pos.idx, bf16[64,4096]{1,0:T(8,128)(2,1)} %collective-permute-done.19.refs_0_, ...), custom_call_target="tpu_custom_call", output_to_operand_aliasing={{1}: (17, {}), {2}: (18, {})} | custom-call | flops 7516192768 | bytes 25165824 | tf_op jit(solution)/shard_map/grads_second/pallas_call | solution.py:263
  177.6 6.4 %collective-permute-done.14 = bf16[128,2048]{1,0:T(8,128)(2,1)S(1)} collective-permute-done((bf16[128,2048]{1,0:T(8,128)(2,1)S(1)}, bf16[128,2048]{1,0:T(8,128)(2,1)S(1)}, u32[]{:S(2)}, u32[]{:S(2)}) %collective-permute-start.14) | collective-permute-done | bytes 524320 | tf_op jit(solution)/shard_map/ppermute | solution.py:41
  184.0 0.7 fusion
  184.7 1.0 pad_maximum_fusion
  (103 shorter events, 3.8 us)
Async XLA Ops:
  2.4 9.8 %collective-permute-start.37 = (bf16[336,128]{1,0:T(8,128)(2,1)S(1)}, bf16[336,128]{1,0:T(8,128)(2,1)S(1)}, u32[]{:S(2)}, u32[]{:S(2)}) collective-permute-start(bf16[336,128]{1,0:T(8,128)(2,1)S(1)} %reshape.46), channel_id=1, source_target_pairs={{0,16},{16,0},{32,48},{48,32},{64,80},{80,64},{96,112},{112,96},{1... | collective-permute-start | bytes 258056 | tf_op jit(solution)/shard_map/ppermute | solution.py:468
  11.0 19.4 %collective-permute-start = (bf16[448,1024]{1,0:T(8,128)(2,1)}, bf16[448,1024]{1,0:T(8,128)(2,1)}, u32[]{:S(2)}, u32[]{:S(2)}) collective-permute-start(bf16[448,1024]{1,0:T(8,128)(2,1)} %get-tuple-element.26.refs_0_), channel_id=1, source_target_pairs={{0,1},{1,0},{2,3},{3,2},{4,5},{5,4},{6,7},{7,6},{8,9},{9,8},{10,11... | collective-permute-start | bytes 2752520 | tf_op jit(solution)/shard_map/ppermute | solution.py:53
  11.1 23.6 %collective-permute-start.1 = (bf16[448,1024]{1,0:T(8,128)(2,1)}, bf16[448,1024]{1,0:T(8,128)(2,1)}, u32[]{:S(2)}, u32[]{:S(2)}) collective-permute-start(bf16[448,1024]{1,0:T(8,128)(2,1)} %get-tuple-element.27), channel_id=1, source_target_pairs={{0,8},{1,9},{2,10},{3,11},{4,12},{5,13},{6,14},{7,15},{8,0},{9,1},... | collective-permute-start | bytes 2752520 | tf_op jit(solution)/shard_map/ppermute | solution.py:49
  12.3 84.6 %copy-start.7 = (bf16[2,336,128]{2,1,0:T(8,128)(2,1)}, bf16[2,336,128]{2,1,0:T(8,128)(2,1)S(1)}, u32[]{:S(2)}) copy-start(bf16[2,336,128]{2,1,0:T(8,128)(2,1)S(1)} %pad_maximum_fusion.1.comp_a) | copy-start | bytes 516100
  12.3 7.8 %collective-permute-start.38 = (bf16[2,336,128]{2,1,0:T(8,128)(2,1)S(1)}, bf16[2,336,128]{2,1,0:T(8,128)(2,1)S(1)}, u32[]{:S(2)}, u32[]{:S(2)}) collective-permute-start(bf16[2,336,128]{2,1,0:T(8,128)(2,1)S(1)} %pad_maximum_fusion.1.comp_a), channel_id=1, source_target_pairs={{0,32},{16,48},{32,64},{48,80},{64,96},{80,112},{96,0},{112,16},{1... | collective-permute-start | bytes 516104 | tf_op jit(solution)/shard_map/ppermute | solution.py:469
  13.9 7.6 %collective-permute-start.39 = (bf16[2,336,128]{2,1,0:T(8,128)(2,1)S(1)}, bf16[2,336,128]{2,1,0:T(8,128)(2,1)S(1)}, u32[]{:S(2)}, u32[]{:S(2)}) collective-permute-start(bf16[2,336,128]{2,1,0:T(8,128)(2,1)S(1)} %pad_maximum_fusion.1.comp_a), channel_id=1, source_target_pairs={{0,96},{16,112},{32,0},{48,16},{64,32},{80,48},{96,64},{112,80},{1... | collective-permute-start | bytes 516104 | tf_op jit(solution)/shard_map/ppermute | solution.py:469
  17.2 24.5 %collective-permute-start.4 = (bf16[112,4096]{1,0:T(8,128)(2,1)S(1)}, bf16[112,4096]{1,0:T(8,128)(2,1)S(1)}, u32[]{:S(2)}, u32[]{:S(2)}) collective-permute-start(bf16[112,4096]{1,0:T(8,128)(2,1)S(1)} %get-tuple-element.47), channel_id=1, source_target_pairs={{0,24},{1,25},{2,26},{3,27},{4,28},{5,29},{6,30},{7,31},{8,16},{9,... | collective-permute-start | bytes 2752520 | tf_op jit(solution)/shard_map/ppermute | solution.py:494
  20.0 76.8 %copy-start.23 = (bf16[2,336,128]{2,1,0:T(8,128)(2,1)}, bf16[2,336,128]{2,1,0:T(8,128)(2,1)S(1)}, u32[]{:S(2)}) copy-start(bf16[2,336,128]{2,1,0:T(8,128)(2,1)S(1)} %collective-permute-done.38.comp_b) | copy-start | bytes 516100
  20.1 25.6 %collective-permute-start.18 = (bf16[128,4096]{1,0:T(8,128)(2,1)S(1)}, bf16[128,4096]{1,0:T(8,128)(2,1)S(1)}, u32[]{:S(2)}, u32[]{:S(2)}) collective-permute-start(bf16[128,4096]{1,0:T(8,128)(2,1)S(1)} %bitcast.75), channel_id=1, source_target_pairs={{0,2},{1,3},{2,4},{3,5},{4,6},{5,7},{6,0},{7,1},{8,10},{9,11},{10,... | collective-permute-start | bytes 3145736 | tf_op jit(solution)/shard_map/ppermute | solution.py:41
  21.5 7.0 %collective-permute-start.40 = (bf16[2,336,128]{2,1,0:T(8,128)(2,1)S(1)}, bf16[2,336,128]{2,1,0:T(8,128)(2,1)}, u32[]{:S(2)}, u32[]{:S(2)}) collective-permute-start(bf16[2,336,128]{2,1,0:T(8,128)(2,1)S(1)} %pad_maximum_fusion.1.comp_a), channel_id=1, source_target_pairs={{0,64},{16,80},{32,96},{48,112},{64,0},{80,16},{96,32},{112,48},{1... | collective-permute-start | bytes 516104 | tf_op jit(solution)/shard_map/ppermute | solution.py:469
  28.6 23.0 %collective-permute-start.20 = (bf16[128,4096]{1,0:T(8,128)(2,1)S(1)}, bf16[128,4096]{1,0:T(8,128)(2,1)S(1)}, u32[]{:S(2)}, u32[]{:S(2)}) collective-permute-start(bf16[128,4096]{1,0:T(8,128)(2,1)S(1)} %bitcast.76), channel_id=1, source_target_pairs={{0,6},{1,7},{2,0},{3,1},{4,2},{5,3},{6,4},{7,5},{8,14},{9,15},{10,... | collective-permute-start | bytes 3145736 | tf_op jit(solution)/shard_map/ppermute | solution.py:45
  30.3 31.3 %collective-permute-start.24 = (bf16[128,4096]{1,0:T(8,128)(2,1)S(1)}, bf16[128,4096]{1,0:T(8,128)(2,1)}, u32[]{:S(2)}, u32[]{:S(2)}) collective-permute-start(bf16[128,4096]{1,0:T(8,128)(2,1)S(1)} %bitcast.77), channel_id=1, source_target_pairs={{0,8},{1,9},{2,10},{3,11},{4,12},{5,13},{6,14},{7,15},{8,0},{9,1},... | collective-permute-start | bytes 3145736 | tf_op jit(solution)/shard_map/ppermute | solution.py:49
  34.7 25.4 %collective-permute-start.7 = (bf16[112,4096]{1,0:T(8,128)(2,1)S(1)}, bf16[112,4096]{1,0:T(8,128)(2,1)S(1)}, u32[]{:S(2)}, u32[]{:S(2)}) collective-permute-start(bf16[112,4096]{1,0:T(8,128)(2,1)S(1)} %get-tuple-element.46), channel_id=1, source_target_pairs={{0,24},{1,25},{2,26},{3,27},{4,28},{5,29},{6,30},{7,31},{8,16},{9,... | collective-permute-start | bytes 2752520 | tf_op jit(solution)/shard_map/ppermute | solution.py:496
  41.7 43.5 %copy-start.11 = (bf16[112,4096]{1,0:T(8,128)(2,1)}, bf16[112,4096]{1,0:T(8,128)(2,1)S(1)}, u32[]{:S(2)}) copy-start(bf16[112,4096]{1,0:T(8,128)(2,1)S(1)} %collective-permute-done.4.refs_6_) | copy-start | bytes 2752516
  41.7 21.7 %collective-permute-start.33 = (bf16[128,4096]{1,0:T(8,128)(2,1)S(1)}, bf16[128,4096]{1,0:T(8,128)(2,1)S(1)}, u32[]{:S(2)}, u32[]{:S(2)}) collective-permute-start(bf16[128,4096]{1,0:T(8,128)(2,1)S(1)} %bitcast.78), channel_id=1, source_target_pairs={{0,1},{1,0},{2,3},{3,2},{4,5},{5,4},{6,7},{7,6},{8,9},{9,8},{10,11... | collective-permute-start | bytes 3145736 | tf_op jit(solution)/shard_map/ppermute | solution.py:53
  45.7 63.5 %copy-start.5 = (bf16[128,4096]{1,0:T(8,128)(2,1)}, bf16[128,4096]{1,0:T(8,128)(2,1)S(1)}, u32[]{:S(2)}) copy-start(bf16[128,4096]{1,0:T(8,128)(2,1)S(1)} %collective-permute-done.18.refs_4_) | copy-start | bytes 3145732
  45.7 74.3 %collective-permute-start.3 = (bf16[448,4096]{1,0:T(8,128)(2,1)}, bf16[448,4096]{1,0:T(8,128)(2,1)}, u32[]{:S(2)}, u32[]{:S(2)}) collective-permute-start(bf16[448,4096]{1,0:T(8,128)(2,1)} %wv.3), channel_id=1, source_target_pairs={{0,1},{1,0},{2,3},{3,2},{4,5},{5,4},{6,7},{7,6},{8,9},{9,8},{10,11... | collective-permute-start | bytes 11010056 | tf_op jit(solution)/shard_map/ppermute | solution.py:53
  51.5 58.1 %copy-start.6 = (bf16[128,4096]{1,0:T(8,128)(2,1)}, bf16[128,4096]{1,0:T(8,128)(2,1)S(1)}, u32[]{:S(2)}) copy-start(bf16[128,4096]{1,0:T(8,128)(2,1)S(1)} %collective-permute-done.20.refs_6_) | copy-start | bytes 3145732
  51.5 24.1 %collective-permute-start.2 = (bf16[448,1024]{1,0:T(8,128)(2,1)}, bf16[448,1024]{1,0:T(8,128)(2,1)S(1)}, u32[]{:S(2)}, u32[]{:S(2)}) collective-permute-start(bf16[448,1024]{1,0:T(8,128)(2,1)} %collective-permute-done.1.refs_2_), channel_id=1, source_target_pairs={{0,1},{1,0},{2,3},{3,2},{4,5},{5,4},{6,7},{7,6},{8,9},{9,8},{10,11... | collective-permute-start | bytes 2752520 | tf_op jit(solution)/shard_map/ppermute | solution.py:53
  60.1 34.4 %copy-start.12 = (bf16[112,4096]{1,0:T(8,128)(2,1)}, bf16[112,4096]{1,0:T(8,128)(2,1)S(1)}, u32[]{:S(2)}) copy-start(bf16[112,4096]{1,0:T(8,128)(2,1)S(1)} %collective-permute-done.7.refs_9_) | copy-start | bytes 2752516
  60.1 14.0 %collective-permute-start.19 = (bf16[64,4096]{1,0:T(8,128)(2,1)S(1)}, bf16[64,4096]{1,0:T(8,128)(2,1)}, u32[]{:S(2)}, u32[]{:S(2)}) collective-permute-start(bf16[64,4096]{1,0:T(8,128)(2,1)S(1)} %slice.18), channel_id=1, source_target_pairs={{0,2},{1,3},{2,4},{3,5},{4,6},{5,7},{6,0},{7,1},{8,10},{9,11},{10,... | collective-permute-start | bytes 1572872 | tf_op jit(solution)/shard_map/ppermute | solution.py:41
  61.6 14.0 %collective-permute-start.21 = (bf16[64,4096]{1,0:T(8,128)(2,1)S(1)}, bf16[64,4096]{1,0:T(8,128)(2,1)}, u32[]{:S(2)}, u32[]{:S(2)}) collective-permute-start(bf16[64,4096]{1,0:T(8,128)(2,1)S(1)} %slice.19), channel_id=1, source_target_pairs={{0,6},{1,7},{2,0},{3,1},{4,2},{5,3},{6,4},{7,5},{8,14},{9,15},{10,... | collective-permute-start | bytes 1572872 | tf_op jit(solution)/shard_map/ppermute | solution.py:45
  63.3 21.9 %collective-permute-start.5 = (bf16[112,4096]{1,0:T(8,128)(2,1)S(1)}, bf16[112,4096]{1,0:T(8,128)(2,1)}, u32[]{:S(2)}, u32[]{:S(2)}) collective-permute-start(bf16[112,4096]{1,0:T(8,128)(2,1)S(1)} %collective-permute-done.4.refs_6_), channel_id=1, source_target_pairs={{0,32},{16,48},{32,64},{48,80},{64,96},{80,112},{96,0},{112,16},{1... | collective-permute-start | bytes 2752520 | tf_op jit(solution)/shard_map/ppermute | solution.py:530
  74.1 20.4 %collective-permute-start.6 = (bf16[112,4096]{1,0:T(8,128)(2,1)S(1)}, bf16[112,4096]{1,0:T(8,128)(2,1)}, u32[]{:S(2)}, u32[]{:S(2)}) collective-permute-start(bf16[112,4096]{1,0:T(8,128)(2,1)S(1)} %collective-permute-done.4.refs_6_), channel_id=1, source_target_pairs={{0,96},{16,112},{32,0},{48,16},{64,32},{80,48},{96,64},{112,80},{1... | collective-permute-start | bytes 2752520 | tf_op jit(solution)/shard_map/ppermute | solution.py:531
  75.6 18.8 %collective-permute-start.8 = (bf16[112,4096]{1,0:T(8,128)(2,1)S(1)}, bf16[112,4096]{1,0:T(8,128)(2,1)S(1)}, u32[]{:S(2)}, u32[]{:S(2)}) collective-permute-start(bf16[112,4096]{1,0:T(8,128)(2,1)S(1)} %collective-permute-done.4.refs_6_), channel_id=1, source_target_pairs={{0,1},{1,0},{2,3},{3,2},{4,5},{5,4},{6,7},{7,6},{8,9},{9,8},{10,11... | collective-permute-start | bytes 2752520 | tf_op jit(solution)/shard_map/ppermute | solution.py:53
  75.7 19.4 %collective-permute-start.11 = (bf16[112,4096]{1,0:T(8,128)(2,1)S(1)}, bf16[112,4096]{1,0:T(8,128)(2,1)S(1)}, u32[]{:S(2)}, u32[]{:S(2)}) collective-permute-start(bf16[112,4096]{1,0:T(8,128)(2,1)S(1)} %collective-permute-done.7.refs_9_), channel_id=1, source_target_pairs={{0,1},{1,0},{2,3},{3,2},{4,5},{5,4},{6,7},{7,6},{8,9},{9,8},{10,11... | collective-permute-start | bytes 2752520 | tf_op jit(solution)/shard_map/ppermute | solution.py:53
  85.2 23.9 %collective-permute-start.25 = (bf16[128,4096]{1,0:T(8,128)(2,1)}, bf16[128,4096]{1,0:T(8,128)(2,1)S(1)}, u32[]{:S(2)}, u32[]{:S(2)}) collective-permute-start(bf16[128,4096]{1,0:T(8,128)(2,1)} %collective-permute-done.24.refs_2_), channel_id=1, source_target_pairs={{0,2},{1,3},{2,4},{3,5},{4,6},{5,7},{6,0},{7,1},{8,10},{9,11},{10,... | collective-permute-start | bytes 3145736 | tf_op jit(solution)/shard_map/ppermute | solution.py:41
  94.5 14.7 %collective-permute-start.9 = (bf16[112,4096]{1,0:T(8,128)(2,1)}, bf16[112,4096]{1,0:T(8,128)(2,1)}, u32[]{:S(2)}, u32[]{:S(2)}) collective-permute-start(bf16[112,4096]{1,0:T(8,128)(2,1)} %collective-permute-done.5.refs_7_), channel_id=1, source_target_pairs={{0,1},{1,0},{2,3},{3,2},{4,5},{5,4},{6,7},{7,6},{8,9},{9,8},{10,11... | collective-permute-start | bytes 2752520 | tf_op jit(solution)/shard_map/ppermute | solution.py:53
  94.5 15.2 %collective-permute-start.10 = (bf16[112,4096]{1,0:T(8,128)(2,1)}, bf16[112,4096]{1,0:T(8,128)(2,1)}, u32[]{:S(2)}, u32[]{:S(2)}) collective-permute-start(bf16[112,4096]{1,0:T(8,128)(2,1)} %collective-permute-done.6.refs_8_), channel_id=1, source_target_pairs={{0,1},{1,0},{2,3},{3,2},{4,5},{5,4},{6,7},{7,6},{8,9},{9,8},{10,11... | collective-permute-start | bytes 2752520 | tf_op jit(solution)/shard_map/ppermute | solution.py:53
  96.3 6.7 %collective-permute-start.22 = (bf16[64,4096]{1,0:T(8,128)(2,1)}, bf16[64,4096]{1,0:T(8,128)(2,1)}, u32[]{:S(2)}, u32[]{:S(2)}) collective-permute-start(bf16[64,4096]{1,0:T(8,128)(2,1)} %collective-permute-done.19.refs_0_), channel_id=1, source_target_pairs={{0,1},{1,0},{2,3},{3,2},{4,5},{5,4},{6,7},{7,6},{8,9},{9,8},{10,11... | collective-permute-start | bytes 1572872 | tf_op jit(solution)/shard_map/ppermute | solution.py:53
  103.1 31.9 %collective-permute-start.27 = (bf16[128,4096]{1,0:T(8,128)(2,1)}, bf16[128,4096]{1,0:T(8,128)(2,1)}, u32[]{:S(2)}, u32[]{:S(2)}) collective-permute-start(bf16[128,4096]{1,0:T(8,128)(2,1)} %collective-permute-done.24.refs_2_), channel_id=1, source_target_pairs={{0,6},{1,7},{2,0},{3,1},{4,2},{5,3},{6,4},{7,5},{8,14},{9,15},{10,... | collective-permute-start | bytes 3145736 | tf_op jit(solution)/shard_map/ppermute | solution.py:45
  109.2 27.9 %copy-start.9 = (bf16[128,4096]{1,0:T(8,128)(2,1)}, bf16[128,4096]{1,0:T(8,128)(2,1)S(1)}, u32[]{:S(2)}) copy-start(bf16[128,4096]{1,0:T(8,128)(2,1)S(1)} %collective-permute-done.25.refs_4_) | copy-start | bytes 3145732
  109.2 28.0 %collective-permute-start.34 = (bf16[128,4096]{1,0:T(8,128)(2,1)}, bf16[128,4096]{1,0:T(8,128)(2,1)}, u32[]{:S(2)}, u32[]{:S(2)}) collective-permute-start(bf16[128,4096]{1,0:T(8,128)(2,1)} %collective-permute-done.24.refs_2_), channel_id=1, source_target_pairs={{0,1},{1,0},{2,3},{3,2},{4,5},{5,4},{6,7},{7,6},{8,9},{9,8},{10,11... | collective-permute-start | bytes 3145736 | tf_op jit(solution)/shard_map/ppermute | solution.py:53
  109.2 28.4 %collective-permute-start.35 = (bf16[128,4096]{1,0:T(8,128)(2,1)S(1)}, bf16[128,4096]{1,0:T(8,128)(2,1)}, u32[]{:S(2)}, u32[]{:S(2)}) collective-permute-start(bf16[128,4096]{1,0:T(8,128)(2,1)S(1)} %collective-permute-done.18.refs_4_), channel_id=1, source_target_pairs={{0,1},{1,0},{2,3},{3,2},{4,5},{5,4},{6,7},{7,6},{8,9},{9,8},{10,11... | collective-permute-start | bytes 3145736 | tf_op jit(solution)/shard_map/ppermute | solution.py:53
  109.7 27.9 %collective-permute-start.36 = (bf16[128,4096]{1,0:T(8,128)(2,1)S(1)}, bf16[128,4096]{1,0:T(8,128)(2,1)}, u32[]{:S(2)}, u32[]{:S(2)}) collective-permute-start(bf16[128,4096]{1,0:T(8,128)(2,1)S(1)} %collective-permute-done.20.refs_6_), channel_id=1, source_target_pairs={{0,1},{1,0},{2,3},{3,2},{4,5},{5,4},{6,7},{7,6},{8,9},{9,8},{10,11... | collective-permute-start | bytes 3145736 | tf_op jit(solution)/shard_map/ppermute | solution.py:53
  120.0 17.0 %collective-permute-start.29 = (bf16[64,4096]{1,0:T(8,128)(2,1)}, bf16[64,4096]{1,0:T(8,128)(2,1)S(1)}, u32[]{:S(2)}, u32[]{:S(2)}) collective-permute-start(bf16[64,4096]{1,0:T(8,128)(2,1)} %collective-permute-done.19.refs_0_), channel_id=1, source_target_pairs={{0,8},{1,9},{2,10},{3,11},{4,12},{5,13},{6,14},{7,15},{8,0},{9,1},... | collective-permute-start | bytes 1572872 | tf_op jit(solution)/shard_map/ppermute | solution.py:49
  134.9 19.6 %collective-permute-start.30 = (bf16[64,4096]{1,0:T(8,128)(2,1)}, bf16[64,4096]{1,0:T(8,128)(2,1)S(1)}, u32[]{:S(2)}, u32[]{:S(2)}) collective-permute-start(bf16[64,4096]{1,0:T(8,128)(2,1)} %collective-permute-done.21.refs_1_), channel_id=1, source_target_pairs={{0,8},{1,9},{2,10},{3,11},{4,12},{5,13},{6,14},{7,15},{8,0},{9,1},... | collective-permute-start | bytes 1572872 | tf_op jit(solution)/shard_map/ppermute | solution.py:49
  137.0 22.0 %collective-permute-start.26 = (bf16[128,4096]{1,0:T(8,128)(2,1)S(1)}, bf16[128,4096]{1,0:T(8,128)(2,1)}, u32[]{:S(2)}, u32[]{:S(2)}) collective-permute-start(bf16[128,4096]{1,0:T(8,128)(2,1)S(1)} %collective-permute-done.25.refs_4_), channel_id=1, source_target_pairs={{0,1},{1,0},{2,3},{3,2},{4,5},{5,4},{6,7},{7,6},{8,9},{9,8},{10,11... | collective-permute-start | bytes 3145736 | tf_op jit(solution)/shard_map/ppermute | solution.py:53
  137.1 25.1 %collective-permute-start.28 = (bf16[128,4096]{1,0:T(8,128)(2,1)}, bf16[128,4096]{1,0:T(8,128)(2,1)}, u32[]{:S(2)}, u32[]{:S(2)}) collective-permute-start(bf16[128,4096]{1,0:T(8,128)(2,1)} %collective-permute-done.27.refs_6_), channel_id=1, source_target_pairs={{0,1},{1,0},{2,3},{3,2},{4,5},{5,4},{6,7},{7,6},{8,9},{9,8},{10,11... | collective-permute-start | bytes 3145736 | tf_op jit(solution)/shard_map/ppermute | solution.py:53
  137.6 17.1 %collective-permute-start.13 = (bf16[128,2048]{1,0:T(8,128)(2,1)}, bf16[128,2048]{1,0:T(8,128)(2,1)S(1)}, u32[]{:S(2)}, u32[]{:S(2)}) collective-permute-start(bf16[128,2048]{1,0:T(8,128)(2,1)} %get-tuple-element.31), channel_id=1, source_target_pairs={{0,2},{1,3},{2,4},{3,5},{4,6},{5,7},{6,0},{7,1},{8,10},{9,11},{10,... | collective-permute-start | bytes 1572872 | tf_op jit(solution)/shard_map/ppermute | solution.py:41
  137.7 17.5 %collective-permute-start.16 = (bf16[128,2048]{1,0:T(8,128)(2,1)}, bf16[128,2048]{1,0:T(8,128)(2,1)S(1)}, u32[]{:S(2)}, u32[]{:S(2)}) collective-permute-start(bf16[128,2048]{1,0:T(8,128)(2,1)} %get-tuple-element.35), channel_id=1, source_target_pairs={{0,6},{1,7},{2,0},{3,1},{4,2},{5,3},{6,4},{7,5},{8,14},{9,15},{10,... | collective-permute-start | bytes 1572872 | tf_op jit(solution)/shard_map/ppermute | solution.py:45
  154.6 2.2 %collective-permute-start.23 = (bf16[64,4096]{1,0:T(8,128)(2,1)}, bf16[64,4096]{1,0:T(8,128)(2,1)S(1)}, u32[]{:S(2)}, u32[]{:S(2)}) collective-permute-start(bf16[64,4096]{1,0:T(8,128)(2,1)} %collective-permute-done.21.refs_1_), channel_id=1, source_target_pairs={{0,1},{1,0},{2,3},{3,2},{4,5},{5,4},{6,7},{7,6},{8,9},{9,8},{10,11... | collective-permute-start | bytes 1572872 | tf_op jit(solution)/shard_map/ppermute | solution.py:53
  154.7 2.8 %collective-permute-start.31 = (bf16[64,4096]{1,0:T(8,128)(2,1)S(1)}, bf16[64,4096]{1,0:T(8,128)(2,1)S(1)}, u32[]{:S(2)}, u32[]{:S(2)}) collective-permute-start(bf16[64,4096]{1,0:T(8,128)(2,1)S(1)} %collective-permute-done.29.refs_8_), channel_id=1, source_target_pairs={{0,1},{1,0},{2,3},{3,2},{4,5},{5,4},{6,7},{7,6},{8,9},{9,8},{10,11... | collective-permute-start | bytes 1572872 | tf_op jit(solution)/shard_map/ppermute | solution.py:53
  155.2 3.7 %collective-permute-start.32 = (bf16[64,4096]{1,0:T(8,128)(2,1)S(1)}, bf16[64,4096]{1,0:T(8,128)(2,1)S(1)}, u32[]{:S(2)}, u32[]{:S(2)}) collective-permute-start(bf16[64,4096]{1,0:T(8,128)(2,1)S(1)} %collective-permute-done.30.refs_9_), channel_id=1, source_target_pairs={{0,1},{1,0},{2,3},{3,2},{4,5},{5,4},{6,7},{7,6},{8,9},{9,8},{10,11... | collective-permute-start | bytes 1572872 | tf_op jit(solution)/shard_map/ppermute | solution.py:53
  156.8 20.8 %collective-permute-start.12 = (bf16[128,2048]{1,0:T(8,128)(2,1)S(1)}, bf16[128,2048]{1,0:T(8,128)(2,1)S(1)}, u32[]{:S(2)}, u32[]{:S(2)}) collective-permute-start(bf16[128,2048]{1,0:T(8,128)(2,1)S(1)} %copy-done.17), channel_id=1, source_target_pairs={{0,6},{1,7},{2,0},{3,1},{4,2},{5,3},{6,4},{7,5},{8,14},{9,15},{10,... | collective-permute-start | bytes 1572872 | tf_op jit(solution)/shard_map/ppermute | solution.py:45
  157.6 20.0 %collective-permute-start.15 = (bf16[128,2048]{1,0:T(8,128)(2,1)S(1)}, bf16[128,2048]{1,0:T(8,128)(2,1)S(1)}, u32[]{:S(2)}, u32[]{:S(2)}) collective-permute-start(bf16[128,2048]{1,0:T(8,128)(2,1)S(1)} %copy-done.16), channel_id=1, source_target_pairs={{0,2},{1,3},{2,4},{3,5},{4,6},{5,7},{6,0},{7,1},{8,10},{9,11},{10,... | collective-permute-start | bytes 1572872 | tf_op jit(solution)/shard_map/ppermute | solution.py:41
  158.9 25.1 %collective-permute-start.14 = (bf16[128,2048]{1,0:T(8,128)(2,1)S(1)}, bf16[128,2048]{1,0:T(8,128)(2,1)S(1)}, u32[]{:S(2)}, u32[]{:S(2)}) collective-permute-start(bf16[128,2048]{1,0:T(8,128)(2,1)S(1)} %add_convert_fusion.3), channel_id=1, source_target_pairs={{0,2},{1,3},{2,4},{3,5},{4,6},{5,7},{6,0},{7,1},{8,10},{9,11},{10,... | collective-permute-start | bytes 1572872 | tf_op jit(solution)/shard_map/ppermute | solution.py:41
  159.0 24.9 %collective-permute-start.17 = (bf16[128,2048]{1,0:T(8,128)(2,1)S(1)}, bf16[128,2048]{1,0:T(8,128)(2,1)S(1)}, u32[]{:S(2)}, u32[]{:S(2)}) collective-permute-start(bf16[128,2048]{1,0:T(8,128)(2,1)S(1)} %add_convert_fusion.1), channel_id=1, source_target_pairs={{0,6},{1,7},{2,0},{3,1},{4,2},{5,3},{6,4},{7,5},{8,14},{9,15},{10,... | collective-permute-start | bytes 1572872 | tf_op jit(solution)/shard_map/ppermute | solution.py:45
  (18 other events, 221.0 us)
